TPU v7x, 256 devices: a 4x2x16 block of a 4x16x16 slice. The times are simulated.
256 devices in a mesh: groups: 2 (over y), bank: 16 (over z), freq: 4 (over x), seg: 2 (over core).
Axes of the slice: x: 4, y: 2, z: 16, core: 2. Of those that a mesh axis runs over, the one named last changes fastest.
The devices are a block of a 4x16x16 slice.
Arguments:
- coarse_spectra: bfloat16 [256, 2, 16384], P(('groups', 'seg', 'bank'), None, 'freq'), parts along dimension 0, may hold values from -6 to 6
- fine_spectra: bfloat16 [256, 2, 65536], P(('groups', 'seg', 'bank'), None, 'freq'), parts along dimension 0, may hold values from -6 to 6
- coarse_templates: bfloat16 [2, 2048, 16384], P(None, 'bank', 'freq'), may hold values from -6 to 6
- fine_templates: bfloat16 [2, 16, 64, 65536], P(None, 'bank', None, 'freq'), may hold values from -6 to 6
- coarse_weight: float32 [32768], P(('groups', 'freq')), parts along dimension 0, may hold values from 0.2 to 2
- fine_weight: float32 [131072], P(('groups', 'freq')), parts along dimension 0, may hold values from 0.2 to 2
- triggers: int32 [256, 2], P(('groups', 'seg')), parts along dimension 0, may hold values from 0 to 15, all different within a row; in each aligned block of 4 rows (0 to 3, 4 to 7, ...) at most 2 rows name the same one
- offsets: int32 [256, 2], P(('groups', 'seg')), parts along dimension 0, may hold values from 0 to 131056
Outputs:
- coarse_snr: float32 [2048, 256], P(('bank', 'freq'), ('groups', 'seg')), parts along dimension 1
- fine_snr: float32 [256, 2, 64], P(('groups', 'seg', 'bank'), None, 'freq'), parts along dimension 0
There are 2 independent parts, one for each index of `groups`. A program takes and returns all parts, laid end to end along the dimension named above; an argument that names none is the same for every part. Nothing has to cross between parts.
Inputs may be any that keep to these rules, and one draw needn't show every extreme that they name: `triggers`: each segment names 2 different sub-banks. In each aligned block of 4 segments (the segments of one device along seg and bank) no sub-bank is named more than 2 times.
All inputs are finite; a program needn't handle non-finite values.
Results may differ from a plain program's by a relative error of at most 0.0021.
Values may be sent and summed in bfloat16 or wider, within the bound.
A program may use at most 128 MiB of HBM per device.

v0:
```python
import math

import jax
import jax.numpy as jnp
from jax import lax
from jax.sharding import PartitionSpec as P

FC = 16384
FB = 65536
CAP = 2
LC = 16
LF = 16
CSTRIDE = 2047


def copy_for_each(x, axis):
    size = lax.axis_size(axis)
    return lax.all_to_all(jnp.broadcast_to(x[None], (size, *x.shape)), axis, 0, 0, tiled=True)


def joined_along(blocks, dim):
    shape = list(blocks.shape[1:])
    shape[dim] *= blocks.shape[0]
    return jnp.moveaxis(blocks, 0, dim).reshape(shape)


def gathered_copies(x, axis, dim):
    blocks = copy_for_each(x, axis)
    return joined_along(blocks, dim)


def in_blocks(x, dim, size):
    shape = x.shape
    blocks = x.reshape(*shape[:dim], size, shape[dim] // size, *shape[dim + 1 :])
    return jnp.moveaxis(blocks, dim, 0)


def sent_and_summed(x, axis, dim):
    blocks = in_blocks(x, dim, lax.axis_size(axis))
    arrived = lax.all_to_all(blocks, axis, split_axis=0, concat_axis=0, tiled=True)
    return arrived.sum(axis=0)


def phase_of(counts, period):
    radians = 2.0 * math.pi / period * counts.astype(jnp.float32)
    return (jnp.cos(radians), jnp.sin(radians))


def offset_count(freq_ids, offset, period):
    upper_bits = offset // 512
    lower_bits = offset % 512
    lower_term = freq_ids * lower_bits % period
    upper_term = freq_ids * upper_bits % (period // 512) * 512
    return (lower_term + upper_term) % period


def lagged(real_part, imag_part, lag_cos, lag_sin):
    left_real = real_part.T[:, :, None]
    left_imag = imag_part.T[:, :, None]
    right_cos = lag_cos[:, None, :]
    right_sin = lag_sin[:, None, :]
    lag_real = (left_real * right_cos - left_imag * right_sin).astype(jnp.bfloat16)
    lag_imag = (left_real * right_sin + left_imag * right_cos).astype(jnp.bfloat16)
    columns = real_part.shape[0] * lag_cos.shape[1]
    return (lag_real.reshape(-1, columns), lag_imag.reshape(-1, columns))


def correlate(temp_real, temp_imag, lag_real, lag_imag):
    corr_real = jnp.dot(temp_real, lag_real, preferred_element_type=jnp.float32) + jnp.dot(
        temp_imag, lag_imag, preferred_element_type=jnp.float32
    )
    corr_imag = jnp.dot(temp_real, lag_imag, preferred_element_type=jnp.float32) - jnp.dot(
        temp_imag, lag_real, preferred_element_type=jnp.float32
    )
    return (corr_real, corr_imag)


def pair_slots(naming, capacity):
    ranking = jnp.cumsum(naming.astype(jnp.int32), axis=1) - 1
    columns = jnp.arange(capacity, dtype=jnp.int32)
    return naming[:, None, :] & (ranking[:, None, :] == columns[None, :, None])


def body(
    coarse_spectra,
    fine_spectra,
    coarse_templates,
    fine_templates,
    coarse_weight,
    fine_weight,
    triggers,
    offsets,
):
    bank_count = lax.axis_size("bank")
    bank_self = lax.axis_index("bank")
    freq_self = lax.axis_index("freq")
    seg_local = fine_spectra.shape[0]
    coarse_bins = coarse_spectra.shape[2]
    fine_bins = fine_spectra.shape[2]
    top_count = triggers.shape[1]
    sub_width = fine_templates.shape[2]
    capacity = CAP
    slot_total = bank_count * capacity
    slot_group = 4
    period_coarse = 2 * FC
    coarse_ids = freq_self * coarse_bins + jnp.arange(coarse_bins, dtype=jnp.int32)
    coarse_lags = jnp.arange(LC, dtype=jnp.int32) * CSTRIDE
    coarse_cos, coarse_sin = phase_of(
        coarse_ids[:, None] * coarse_lags[None, :] % period_coarse, period_coarse
    )
    temp_real = coarse_templates[0]
    temp_imag = coarse_templates[1]
    coarse_partial = jnp.sum(
        (temp_real.astype(jnp.float32) ** 2 + temp_imag.astype(jnp.float32) ** 2)
        * coarse_weight[None, :],
        axis=1,
    )
    weighted = (
        gathered_copies(coarse_spectra, "bank", 0).astype(jnp.float32)
        * coarse_weight[None, None, :]
    )
    lag_real, lag_imag = lagged(weighted[:, 0], weighted[:, 1], coarse_cos, coarse_sin)
    corr_real, corr_imag = correlate(temp_real, temp_imag, lag_real, lag_imag)
    coarse_corr = jnp.stack([corr_real, corr_imag])
    coarse_corr, coarse_norm = (
        sent_and_summed(coarse_corr, "freq", 1),
        sent_and_summed(coarse_partial[None, :], "freq", 1),
    )
    coarse_energy = coarse_corr[0] * coarse_corr[0] + coarse_corr[1] * coarse_corr[1]
    coarse_rows = coarse_energy.shape[0]
    coarse_snr = (
        jnp.max(coarse_energy.reshape(coarse_rows, -1, LC), axis=2) / coarse_norm[0][:, None]
    )
    trig_blocks = triggers.reshape(bank_count, seg_local * top_count)
    offset_blocks = offsets.reshape(bank_count, seg_local * top_count)
    recv_pairs = pair_slots(trig_blocks == bank_self, capacity)
    recv_segments = jnp.any(recv_pairs.reshape(bank_count, capacity, seg_local, top_count), axis=3)
    slot_offsets = jnp.sum(jnp.where(recv_pairs, offset_blocks[:, None, :], 0), axis=2).reshape(-1)
    everything = lax.all_gather(fine_spectra, "bank", axis=0, tiled=True)
    incoming = jnp.einsum(
        "dcs,dsx->dcx",
        recv_segments.astype(jnp.bfloat16),
        everything.reshape(bank_count, seg_local, -1),
        preferred_element_type=jnp.float32,
    ).astype(jnp.bfloat16)
    slots = incoming.reshape(slot_total, 2, fine_bins)
    period_fine = 2 * FB
    fine_ids = freq_self * fine_bins + jnp.arange(fine_bins, dtype=jnp.int32)
    fine_lags = jnp.arange(LF, dtype=jnp.int32)
    fine_cos, fine_sin = phase_of(fine_ids[:, None] * fine_lags[None, :] % period_fine, period_fine)
    sub_real = fine_templates[0, 0]
    sub_imag = fine_templates[1, 0]
    fine_partial = jnp.sum(
        (sub_real.astype(jnp.float32) ** 2 + sub_imag.astype(jnp.float32) ** 2)
        * fine_weight[None, :],
        axis=1,
    )

    def fine_block(slot_rows, row_offsets):
        weighted = slot_rows.astype(jnp.float32) * fine_weight[None, None, :]
        shift_cos, shift_sin = phase_of(
            offset_count(fine_ids[None, :], row_offsets[:, None], period_fine), period_fine
        )
        shifted_real = weighted[:, 0] * shift_cos - weighted[:, 1] * shift_sin
        shifted_imag = weighted[:, 0] * shift_sin + weighted[:, 1] * shift_cos
        lag_real, lag_imag = lagged(shifted_real, shifted_imag, fine_cos, fine_sin)
        corr_real, corr_imag = correlate(sub_real, sub_imag, lag_real, lag_imag)
        return jnp.stack([corr_real, corr_imag])

    grouped = slots.reshape(slot_total // slot_group, slot_group, 2, fine_bins)
    grouped_offsets = slot_offsets.reshape(slot_total // slot_group, slot_group)

    def run_group(pair):
        return fine_block(pair[0], pair[1])

    pieces = lax.map(run_group, (grouped, grouped_offsets))
    fine_corr = jnp.transpose(pieces, (1, 2, 0, 3)).reshape(2, sub_width, slot_total * LF)
    fine_corr, fine_norm = (
        sent_and_summed(fine_corr, "freq", 1),
        sent_and_summed(fine_partial[None, :], "freq", 1),
    )
    fine_energy = fine_corr[0] * fine_corr[0] + fine_corr[1] * fine_corr[1]
    quarter = fine_energy.shape[0]
    slot_snr = (
        jnp.max(fine_energy.reshape(quarter, slot_total, LF), axis=2) / fine_norm[0][:, None]
    ).T
    slot_snr = slot_snr.reshape(bank_count, capacity, quarter)
    spread = jnp.einsum(
        "dcp,dct->dpt", recv_pairs.astype(jnp.float32), slot_snr, precision=lax.Precision.HIGHEST
    )
    fine_rows = sent_and_summed(spread, "bank", 0)[0]
    fine_snr = fine_rows.reshape(seg_local, top_count, quarter)
    return (coarse_snr, fine_snr)


def solution(mesh):
    return jax.shard_map(
        body,
        mesh=mesh,
        in_specs=(
            P(("groups", "seg", "bank"), None, "freq"),
            P(("groups", "seg", "bank"), None, "freq"),
            P(None, "bank", "freq"),
            P(None, "bank", None, "freq"),
            P(("groups", "freq")),
            P(("groups", "freq")),
            P(("groups", "seg"), None),
            P(("groups", "seg"), None),
        ),
        out_specs=(
            P(("bank", "freq"), ("groups", "seg")),
            P(("groups", "seg", "bank"), None, "freq"),
        ),
        check_vma=False,
    )
```

profile of v0, /device:TPU:40, one launch (start us, length us, event | category | flops | bytes accessed | tf_op | source)
XLA Modules:
  0.0 313.2 jit_solution(16488393959525336833)
XLA Ops:
  8.2 1.4 broadcast_in_dim.27
  9.7 24.1 %all-to-all-start = ((bf16[16,4,2,4096]{3,1,2,0:T(4,128)(2,1)}), bf16[16,4,2,4096]{3,1,2,0:T(4,128)(2,1)S(1)}, u32[]{:S(2)}, u32[]{:S(2)}) async-start(bf16[16,4,2,4096]{3,1,2,0:T(4,128)(2,1)} %broadcast_in_dim.27), calls=%async_computation | async-start | bytes 2097152 | tf_op jit(solution)/shard_map/all_to_all | solution.py:18
  35.9 1.8 fusion.42
  37.7 3.3 %multiply_reduce_fusion = f32[64]{0:T(128)S(1)} fusion(f32[16384]{0:T(1024)S(1)} %copy-done.1, bf16[2,1,64,16384]{3,2,1,0:T(8,128)(2,1)} %param.13), kind=kLoop, calls=%fused_computation.62 | loop fusion | flops 7339968 | bytes 4260096 | tf_op jit(solution)/shard_map/reduce_sum | solution.py:153
  41.7 3.9 %slice_bitcast_fusion.2 = (bf16[64,16384]{1,0:T(8,128)(2,1)S(1)}, bf16[64,16384]{1,0:T(8,128)(2,1)}) fusion(bf16[2,1,64,16384]{3,2,1,0:T(8,128)(2,1)} %param.13), kind=kLoop, calls=%fused_computation.64 | loop fusion | bytes 8388608 | tf_op jit(solution)/shard_map/squeeze | solution.py:152
  45.6 44.7 %all-to-all-done = bf16[16,4,2,4096]{3,1,2,0:T(4,128)(2,1)S(1)} async-done(((bf16[16,4,2,4096]{3,1,2,0:T(4,128)(2,1)}), bf16[16,4,2,4096]{3,1,2,0:T(4,128)(2,1)S(1)}, u32[]{:S(2)}, u32[]{:S(2)}) %all-to-all-start) | async-done | bytes 1048608 | tf_op jit(solution)/shard_map/all_to_all | solution.py:18
  90.3 4.7 %all-to-all-start.4 = ((f32[4,1,16]{2,1,0:T(1,128)}), f32[4,1,16]{2,1,0:T(1,128)S(1)}, u32[]{:S(2)}, u32[]{:S(2)}) async-start(f32[4,1,16]{2,1,0:T(1,128)} %bitcast.22), calls=%async_computation.4 | async-start | bytes 4096 | tf_op jit(solution)/shard_map/all_to_all | solution.py:40
  95.6 1.6 copy.102
  98.2 2.4 fusion.50
  100.6 1.6 copy_bitcast_fusion.1
  102.3 6.1 %subtract_convert_fusion.1 = (bf16[4096,64,16]{0,2,1:T(8,128)(2,1)S(1)}, bf16[4096,64,16]{0,2,1:T(8,128)(2,1)S(1)}) fusion(f32[4096,16]{0,1:T(8,128)S(1)} %copy-done.4, f32[4096,64]{0,1:T(8,128)S(1)} %get-tuple-element.312, f32[4096,16]{0,1:T(8,128)S(1)} %get-tuple-element.308, f32[4096,64]{0,1:T(8,128)S(1)} %get-tuple-element.313), kind=kLoop, calls=%fused_computation.61 | loop fusion | flops 33554432 | bytes 19398656 | tf_op jit(solution)/shard_map/convert_element_type | solution.py:62
  108.4 2.9 fusion.31
  111.3 2.9 fusion.29
  114.2 2.9 convolution_add_fusion.1
  117.1 2.9 convolution_subtract_fusion.1
  120.0 4.8 %all-to-all-start.2 = ((f32[4,1,32]{2,1,0:T(1,128)}), f32[4,1,32]{2,1,0:T(1,128)S(1)}, u32[]{:S(2)}, u32[]{:S(2)}) async-start(f32[4,1,32]{2,1,0:T(1,128)} %bitcast.15), calls=%async_computation.2 | async-start | bytes 4096 | tf_op jit(solution)/shard_map/all_to_all | solution.py:40
  125.8 4.2 %all-to-all-done.2 = f32[4,1,32]{2,1,0:T(1,128)S(1)} async-done(((f32[4,1,32]{2,1,0:T(1,128)}), f32[4,1,32]{2,1,0:T(1,128)S(1)}, u32[]{:S(2)}, u32[]{:S(2)}) %all-to-all-start.2) | async-done | bytes 544 | tf_op jit(solution)/shard_map/all_to_all | solution.py:40
  130.0 3.6 %all-to-all-start.1 = ((f32[4,2,32,1024]{3,2,1,0:T(8,128)}), f32[4,2,32,1024]{3,2,1,0:T(8,128)S(1)}, u32[]{:S(2)}, u32[]{:S(2)}) async-start(f32[4,2,32,1024]{3,2,1,0:T(8,128)} %maximum_bitcast_fusion.1), calls=%async_computation.1 | async-start | bytes 2097152 | tf_op jit(solution)/shard_map/all_to_all | solution.py:40
  135.8 1.3 reduce_sum.78
  137.6 6.8 %all-to-all-done.1 = f32[4,2,32,1024]{3,2,1,0:T(8,128)S(1)} async-done(((f32[4,2,32,1024]{3,2,1,0:T(8,128)}), f32[4,2,32,1024]{3,2,1,0:T(8,128)S(1)}, u32[]{:S(2)}, u32[]{:S(2)}) %all-to-all-start.1) | async-done | bytes 1048608 | tf_op jit(solution)/shard_map/all_to_all | solution.py:40
  144.5 7.6 %reshape.351 = bf16[16,4,32768]{2,1,0:T(4,128)(2,1)} reshape(bf16[64,2,16384]{2,1,0:T(2,128)(2,1)} %all-gather.2.cloned.1.call-done) | data formatting | bytes 8388608 | tf_op jit(solution)/shard_map/reshape | solution.py:143
  152.1 5.8 %convolution_convert_fusion = bf16[16,2,32768]{2,1,0:T(2,128)(2,1)} fusion(pred[16,2,4]{2,1,0:T(4,128)(4,1)S(1)} %copy-done.7, bf16[16,4,32768]{2,1,0:T(4,128)(2,1)} %reshape.351), kind=kOutput, calls=%fused_computation.59 | convolution fusion | flops 9437184 | bytes 6291584 | tf_op jit(solution)/shard_map/dcs,dsx->dcx/dot_general | solution.py:140
  158.0 7.2 %reshape_reshape.9 = bf16[8,4,2,16384]{3,2,1,0:T(2,128)(2,1)} reshape(bf16[16,2,32768]{2,1,0:T(2,128)(2,1)} %convolution_convert_fusion) | data formatting | bytes 4194304 | tf_op jit(solution)/shard_map/reshape;reshape | solution.py:170
  165.2 102.6 %while.15 = (s32[]{:T(128)}, f32[8,2,64,64]{2,3,1,0:T(8,128)S(1)}, bf16[8,4,2,16384]{3,2,1,0:T(2,128)(2,1)}, f32[16384]{0:T(1024)S(1)}, s32[8,4]{1,0:T(8,128)S(1...) while((s32[]{:T(128)}, f32[8,2,64,64]{2,3,1,0:T(8,128)S(1)}, ...), condition=%wide.region_8.9_spmd.clone.clone, body=%wide.region_7.8_spmd.clone.clone.sunk | while | flops 552173696 | bytes 36929812 | solution.py:176
  165.5 1.1 constant_dynamic-slice_fusion.3
  166.9 2.8 subtract_bitcast_fusion.2
  169.7 4.1 %fusion.90 = (f32[16384,16]{0,1:T(8,128)S(1)}, f32[16384,16]{0,1:T(8,128)S(1)}) fusion(s32[16384]{0:T(1024)S(1)} %get-tuple-element.413), kind=kLoop, calls=%fused_computation.20.clone.1 | loop fusion | flops 3670016 | bytes 2162688 | tf_op jit(solution)/shard_map/cos | solution.py:46
  178.3 1.1 constant_dynamic-slice_fusion.3
  179.7 2.8 subtract_bitcast_fusion.2
  182.5 4.1 %fusion.90 = (f32[16384,16]{0,1:T(8,128)S(1)}, f32[16384,16]{0,1:T(8,128)S(1)}) fusion(s32[16384]{0:T(1024)S(1)} %get-tuple-element.413), kind=kLoop, calls=%fused_computation.20.clone.1 | loop fusion | flops 3670016 | bytes 2162688 | tf_op jit(solution)/shard_map/cos | solution.py:46
  191.1 1.1 constant_dynamic-slice_fusion.3
  192.5 2.8 subtract_bitcast_fusion.2
  195.2 4.1 %fusion.90 = (f32[16384,16]{0,1:T(8,128)S(1)}, f32[16384,16]{0,1:T(8,128)S(1)}) fusion(s32[16384]{0:T(1024)S(1)} %get-tuple-element.413), kind=kLoop, calls=%fused_computation.20.clone.1 | loop fusion | flops 3670016 | bytes 2162688 | tf_op jit(solution)/shard_map/cos | solution.py:46
  203.9 1.1 constant_dynamic-slice_fusion.3
  205.3 2.8 subtract_bitcast_fusion.2
  208.0 4.1 %fusion.90 = (f32[16384,16]{0,1:T(8,128)S(1)}, f32[16384,16]{0,1:T(8,128)S(1)}) fusion(s32[16384]{0:T(1024)S(1)} %get-tuple-element.413), kind=kLoop, calls=%fused_computation.20.clone.1 | loop fusion | flops 3670016 | bytes 2162688 | tf_op jit(solution)/shard_map/cos | solution.py:46
  218.1 2.8 subtract_bitcast_fusion.2
  220.8 4.1 %fusion.90 = (f32[16384,16]{0,1:T(8,128)S(1)}, f32[16384,16]{0,1:T(8,128)S(1)}) fusion(s32[16384]{0:T(1024)S(1)} %get-tuple-element.413), kind=kLoop, calls=%fused_computation.20.clone.1 | loop fusion | flops 3670016 | bytes 2162688 | tf_op jit(solution)/shard_map/cos | solution.py:46
  230.9 2.8 subtract_bitcast_fusion.2
  233.6 4.1 %fusion.90 = (f32[16384,16]{0,1:T(8,128)S(1)}, f32[16384,16]{0,1:T(8,128)S(1)}) fusion(s32[16384]{0:T(1024)S(1)} %get-tuple-element.413), kind=kLoop, calls=%fused_computation.20.clone.1 | loop fusion | flops 3670016 | bytes 2162688 | tf_op jit(solution)/shard_map/cos | solution.py:46
  243.7 2.8 subtract_bitcast_fusion.2
  246.4 4.1 %fusion.90 = (f32[16384,16]{0,1:T(8,128)S(1)}, f32[16384,16]{0,1:T(8,128)S(1)}) fusion(s32[16384]{0:T(1024)S(1)} %get-tuple-element.413), kind=kLoop, calls=%fused_computation.20.clone.1 | loop fusion | flops 3670016 | bytes 2162688 | tf_op jit(solution)/shard_map/cos | solution.py:46
  256.5 2.8 subtract_bitcast_fusion.2
  259.2 4.1 %fusion.90 = (f32[16384,16]{0,1:T(8,128)S(1)}, f32[16384,16]{0,1:T(8,128)S(1)}) fusion(s32[16384]{0:T(1024)S(1)} %get-tuple-element.413), kind=kLoop, calls=%fused_computation.20.clone.1 | loop fusion | flops 3670016 | bytes 2162688 | tf_op jit(solution)/shard_map/cos | solution.py:46
  268.9 3.5 %all-to-all-start.3 = ((f32[4,2,16,512]{3,2,1,0:T(8,128)}), f32[4,2,16,512]{3,2,1,0:T(8,128)S(1)}, u32[]{:S(2)}, u32[]{:S(2)}) async-start(f32[4,2,16,512]{3,2,1,0:T(8,128)} %copy.119), calls=%async_computation.3 | async-start | bytes 524288 | tf_op jit(solution)/shard_map/all_to_all | solution.py:40
  272.8 6.2 %all-to-all-done.3 = f32[4,2,16,512]{3,2,1,0:T(8,128)S(1)} async-done(((f32[4,2,16,512]{3,2,1,0:T(8,128)}), f32[4,2,16,512]{3,2,1,0:T(8,128)S(1)}, u32[]{:S(2)}, u32[]{:S(2)}) %all-to-all-start.3) | async-done | bytes 262176 | tf_op jit(solution)/shard_map/all_to_all | solution.py:40
  280.4 11.3 %all-to-all-start.5 = ((f32[16,1,128]{2,1,0:T(1,128)}), f32[16,1,128]{2,1,0:T(1,128)S(1)}, u32[]{:S(2)}, u32[]{:S(2)}) async-start(f32[16,1,128]{2,1,0:T(1,128)} %reshape.359), calls=%async_computation.5 | async-start | bytes 16384 | tf_op jit(solution)/shard_map/all_to_all | solution.py:40
  292.5 11.6 %all-to-all-done.5 = f32[16,1,128]{2,1,0:T(1,128)S(1)} async-done(((f32[16,1,128]{2,1,0:T(1,128)}), f32[16,1,128]{2,1,0:T(1,128)S(1)}, u32[]{:S(2)}, u32[]{:S(2)}) %all-to-all-start.5) | async-done | bytes 8224 | tf_op jit(solution)/shard_map/all_to_all | solution.py:40
  (178 shorter events, 57.0 us)
Async XLA Ops:
  7.2 27.5 %copy-start.6 = (f32[4096]{0:T(1024)S(1)}, f32[4096]{0:T(1024)}, u32[]{:S(2)}) copy-start(f32[4096]{0:T(1024)} %param.14) | copy-start | bytes 49156
  7.2 27.5 %copy-start.2 = (bf16[2,128,4096]{2,1,0:T(8,128)(2,1)S(1)}, bf16[2,128,4096]{2,1,0:T(8,128)(2,1)}, u32[]{:S(2)}) copy-start(bf16[2,128,4096]{2,1,0:T(8,128)(2,1)} %param.12) | copy-start | bytes 6291460
  9.7 28.0 %copy-start.1 = (f32[16384]{0:T(1024)S(1)}, f32[16384]{0:T(1024)}, u32[]{:S(2)}) copy-start(f32[16384]{0:T(1024)} %param.15) | copy-start | bytes 196612
  9.7 80.6 %all-to-all-start = ((bf16[16,4,2,4096]{3,1,2,0:T(4,128)(2,1)}), bf16[16,4,2,4096]{3,1,2,0:T(4,128)(2,1)S(1)}, u32[]{:S(2)}, u32[]{:S(2)}) async-start(bf16[16,4,2,4096]{3,1,2,0:T(4,128)(2,1)} %broadcast_in_dim.27), calls=%async_computation | async-start | bytes 2097152 | tf_op jit(solution)/shard_map/all_to_all | solution.py:18
  33.8 110.7 %all-gather.2.cloned.1.call-start = ((), (), s32[]{:S(2)}) async-start(), calls=%async_computation.6 | async-start | bytes 4456448 | tf_op jit(solution)/shard_map/all_gather | solution.py:139
  90.3 29.6 %all-to-all-start.4 = ((f32[4,1,16]{2,1,0:T(1,128)}), f32[4,1,16]{2,1,0:T(1,128)S(1)}, u32[]{:S(2)}, u32[]{:S(2)}) async-start(f32[4,1,16]{2,1,0:T(1,128)} %bitcast.22), calls=%async_computation.4 | async-start | bytes 4096 | tf_op jit(solution)/shard_map/all_to_all | solution.py:40
  100.6 1.7 copy-start.4
  102.3 6.1 %copy-start.3 = (bf16[2,128,4096]{2,1,0:T(8,128)(2,1)S(1)}, bf16[2,128,4096]{2,1,0:T(8,128)(2,1)}, u32[]{:S(2)}) copy-start(bf16[2,128,4096]{2,1,0:T(8,128)(2,1)} %param.12) | copy-start | bytes 6291460
  120.0 10.0 %copy-start.8 = (f32[4,1,16]{2,1,0:T(1,128)}, f32[4,1,16]{2,1,0:T(1,128)S(1)}, u32[]{:S(2)}) copy-start(f32[4,1,16]{2,1,0:T(1,128)S(1)} %all-to-all-done.4) | copy-start | bytes 772
  120.0 10.0 %all-to-all-start.2 = ((f32[4,1,32]{2,1,0:T(1,128)}), f32[4,1,32]{2,1,0:T(1,128)S(1)}, u32[]{:S(2)}, u32[]{:S(2)}) async-start(f32[4,1,32]{2,1,0:T(1,128)} %bitcast.15), calls=%async_computation.2 | async-start | bytes 4096 | tf_op jit(solution)/shard_map/all_to_all | solution.py:40
  124.8 8.8 %copy-start.11 = (s32[64,2]{0,1:T(2,128)S(1)}, s32[64,2]{0,1:T(2,128)}, u32[]{:S(2)}) copy-start(s32[64,2]{0,1:T(2,128)} %param.16) | copy-start | bytes 1540
  124.8 9.3 %copy-start.12 = (s32[64,2]{0,1:T(2,128)S(1)}, s32[64,2]{0,1:T(2,128)}, u32[]{:S(2)}) copy-start(s32[64,2]{0,1:T(2,128)} %param.17) | copy-start | bytes 1540
  130.0 14.4 %all-to-all-start.1 = ((f32[4,2,32,1024]{3,2,1,0:T(8,128)}), f32[4,2,32,1024]{3,2,1,0:T(8,128)S(1)}, u32[]{:S(2)}, u32[]{:S(2)}) async-start(f32[4,2,32,1024]{3,2,1,0:T(8,128)} %maximum_bitcast_fusion.1), calls=%async_computation.1 | async-start | bytes 2097152 | tf_op jit(solution)/shard_map/all_to_all | solution.py:40
  144.5 7.7 %copy-start.7 = (pred[16,2,4]{2,1,0:T(4,128)(4,1)S(1)}, pred[16,2,4]{2,1,0:T(4,128)(4,1)}, u32[]{:S(2)}) copy-start(pred[16,2,4]{2,1,0:T(4,128)(4,1)} %copy.115) | copy-start | bytes 388
  158.0 7.2 %copy-start.5 = (f32[8,2,64,64]{2,3,1,0:T(8,128)S(1)}, f32[8,2,64,64]{2,3,1,0:T(8,128)}, u32[]{:S(2)}) copy-start(f32[8,2,64,64]{2,3,1,0:T(8,128)} %custom-call) | copy-start | bytes 786436
  173.7 1.6 copy-start
  186.5 1.6 copy-start
  199.3 1.6 copy-start
  212.1 1.6 copy-start
  224.9 1.6 copy-start
  237.7 1.6 copy-start
  250.5 1.6 copy-start
  263.3 1.6 copy-start
  268.1 11.3 %copy-start.10 = (f32[16]{0:T(128)S(1)}, f32[16]{0:T(128)}, u32[]{:S(2)}) copy-start(f32[16]{0:T(128)} %reduce_sum.78) | copy-start | bytes 196
  268.2 23.5 %copy-start.9 = (f32[32]{0:T(128)S(1)}, f32[32]{0:T(128)}, u32[]{:S(2)}) copy-start(f32[32]{0:T(128)} %reduce_sum.74) | copy-start | bytes 388
  268.9 10.1 %all-to-all-start.3 = ((f32[4,2,16,512]{3,2,1,0:T(8,128)}), f32[4,2,16,512]{3,2,1,0:T(8,128)S(1)}, u32[]{:S(2)}, u32[]{:S(2)}) async-start(f32[4,2,16,512]{3,2,1,0:T(8,128)} %copy.119), calls=%async_computation.3 | async-start | bytes 524288 | tf_op jit(solution)/shard_map/all_to_all | solution.py:40
  280.4 23.6 %all-to-all-start.5 = ((f32[16,1,128]{2,1,0:T(1,128)}), f32[16,1,128]{2,1,0:T(1,128)S(1)}, u32[]{:S(2)}, u32[]{:S(2)}) async-start(f32[16,1,128]{2,1,0:T(1,128)} %reshape.359), calls=%async_computation.5 | async-start | bytes 16384 | tf_op jit(solution)/shard_map/all_to_all | solution.py:40
Sparse Core Ops, SparseCore 0:
  36.4 101.3 all-gather.1
where the time goes:
time: 318 us; the launch traced here: 313 us
  other arithmetic  83.4 us (26%)
  waiting for transfers between devices  74.2 us (23%)
  starting transfers between devices  52.1 us (16%)
  local copies, waits for them, and re-layouts  47.1 us (15%)
  matrix products  40.5 us (13%)
  between operations  14.9 us (5%)
    all_to_all x1, waiting for transfers between devices, copy_for_each(): lax.all_to_all(jnp.broadcast_to(x[None], (size, *x.shape)), axis, 0, 0, t...  44.7 us
    cos x9, other arithmetic, phase_of(): return (jnp.cos(radians), jnp.sin(radians))  34.3 us
    all_to_all x5, waiting for transfers between devices, sent_and_summed(): lax.all_to_all(blocks, axis, split_axis=0, concat_axis=0, tiled=True)  28.8 us
    all_to_all x5, starting transfers between devices, sent_and_summed(): lax.all_to_all(blocks, axis, split_axis=0, concat_axis=0, tiled=True)  27.9 us
    all_to_all x1, starting transfers between devices, copy_for_each(): lax.all_to_all(jnp.broadcast_to(x[None], (size, *x.shape)), axis, 0, 0, t...  24.1 us
    transpose x8, other arithmetic, lagged(): left_real = real_part.T[:, :, None]  22 us
    convert_element_type x9, other arithmetic, lagged(): (left_real * right_cos - left_imag * right_sin).astype(jnp.bfloat16)  14.1 us
    dot_general x9, matrix products, correlate(): jnp.dot(temp_imag, lag_imag, preferred_element_type=jnp.float32)  9.24 us
  transfers between devices with their start and end apart: 7, of which 5 were waited for; matrix products, arithmetic and copies ran while one was open for 13% of the time, Pallas kernels for 0%

commit v1 on v0

v1 whole, which is shorter than its diff:
```python
import functools
import math

import jax
import jax.numpy as jnp
from jax import lax
from jax.experimental import pallas as pl
from jax.experimental.pallas import tpu as pltpu
from jax.sharding import PartitionSpec as P

FC = 16384
FB = 65536
CAP = 2
LC = 16
LF = 16
CSTRIDE = 2047
PERIOD = 131072
STEP = 512
LANES = 128
MESH = pl.DeviceIdType.MESH
NT = (((1,), (1,)), ((), ()))
NN = (((1,), (0,)), ((), ()))


def unit_phase(count):
    quadrant = (count + PERIOD // 8) >> 15
    x = (count - (quadrant << 15)).astype(jnp.float32) * (2.0 * math.pi / PERIOD)
    z = x * x
    s = x * (1.0 + z * (-1.0 / 6 + z * (1.0 / 120 + z * (-1.0 / 5040 + z * (1.0 / 362880)))))
    c = 1.0 + z * (-0.5 + z * (1.0 / 24 + z * (-1.0 / 720 + z * (1.0 / 40320 - z * (1.0 / 3628800)))))
    odd = (quadrant & 1) == 1
    cos = jnp.where(odd, s, c)
    sin = jnp.where(odd, c, s)
    cos = jnp.where(((quadrant + 1) & 2) == 2, -cos, cos)
    sin = jnp.where((quadrant & 2) == 2, -sin, sin)
    return cos, sin


def kernel(
    nb,
    nf,
    trig,
    offs,
    cs_hbm,
    fs_hbm,
    ct_hbm,
    ft_hbm,
    cw,
    fw,
    coarse_out,
    fine_out,
    cbuf,
    fbuf,
    ct,
    ft,
    ctab,
    ftab,
    clag,
    flag,
    cpq,
    fpq,
    sel,
    soff,
    cstage,
    crecv,
    fstage,
    frecv,
    nstage,
    nrecv,
    cnorm,
    fnorm,
    cres,
    rstage,
    rrecv,
    load_sem,
    ct_sem,
    ft_sem,
    c_send,
    c_recv,
    f_send,
    f_recv,
    n_send,
    n_recv,
    cx_send,
    cx_recv,
    fx_send,
    fx_recv,
    r_send,
    r_recv,
):
    me = lax.axis_index("bank")
    fx = lax.axis_index("freq")
    groups = nb // 4
    segs = cbuf.shape[1] // 2
    cbins = cbuf.shape[2]
    fbins = fbuf.shape[2]
    parts = f_send.shape[1]
    fpart = fbins // parts
    ctn = ct.shape[0] // 2
    ftn = ft.shape[0] // 2
    cq = ctn // nf
    fq = ftn // nf
    scale = PERIOD // (2 * FC)

    def source(p):
        step = (nb - (p + 1) // 2) if p % 2 else p // 2
        return lax.rem(me + step, nb)

    def other(k):
        return lax.rem(fx + k, nf)

    right = lax.rem(me + 1, nb)
    left = lax.rem(me + nb - 1, nb)

    def c_move(p):
        return pltpu.make_async_remote_copy(
            src_ref=cbuf.at[max(p - 2, 0)],
            dst_ref=cbuf.at[p],
            send_sem=c_send.at[p],
            recv_sem=c_recv.at[p],
            device_id={"bank": right if p % 2 else left},
            device_id_type=MESH,
        )

    def f_move(p, c):
        last = p == nb - 1
        leftward = p % 2 == 0 or (last and c >= parts // 2)
        origin = p - 1 if (last and leftward) else max(p - 2, 0)
        part = pl.ds(c * fpart, fpart)
        return pltpu.make_async_remote_copy(
            src_ref=fbuf.at[origin, :, part],
            dst_ref=fbuf.at[p, :, part],
            send_sem=f_send.at[p, c],
            recv_sem=f_recv.at[p, c],
            device_id={"bank": left if leftward else right},
            device_id_type=MESH,
        )

    def n_move(k):
        return pltpu.make_async_remote_copy(
            src_ref=nstage.at[other(k)],
            dst_ref=nrecv.at[k - 1],
            send_sem=n_send.at[k - 1],
            recv_sem=n_recv.at[k - 1],
            device_id={"freq": other(k)},
            device_id_type=MESH,
        )

    def cx_move(g, k):
        return pltpu.make_async_remote_copy(
            src_ref=cstage.at[g, other(k)],
            dst_ref=crecv.at[g, k - 1],
            send_sem=cx_send.at[g, k - 1],
            recv_sem=cx_recv.at[g, k - 1],
            device_id={"freq": other(k)},
            device_id_type=MESH,
        )

    def fx_move(g, k):
        return pltpu.make_async_remote_copy(
            src_ref=fstage.at[g, other(k)],
            dst_ref=frecv.at[g, k - 1],
            send_sem=fx_send.at[g, k - 1],
            recv_sem=fx_recv.at[g, k - 1],
            device_id={"freq": other(k)},
            device_id_type=MESH,
        )

    def r_move(p):
        return pltpu.make_async_remote_copy(
            src_ref=rstage.at[p // 4],
            dst_ref=rrecv.at[p],
            send_sem=r_send.at[p],
            recv_sem=r_recv.at[p],
            device_id={"bank": source(p)},
            device_id_type=MESH,
        )

    own_c = pltpu.make_async_copy(cs_hbm, cbuf.at[0], load_sem.at[0])
    own_f = pltpu.make_async_copy(fs_hbm, fbuf.at[0], load_sem.at[1])
    own_c.start()
    own_f.start()
    load_ct = pltpu.make_async_copy(ct_hbm, ct, ct_sem)
    load_ft = pltpu.make_async_copy(ft_hbm, ft, ft_sem)
    load_ct.start()
    load_ft.start()

    barrier = pltpu.get_barrier_semaphore()
    for neighbour in (left, right):
        pl.semaphore_signal(barrier, inc=1, device_id={"bank": neighbour}, device_id_type=MESH)
    for k in range(1, nf):
        pl.semaphore_signal(barrier, inc=1, device_id={"freq": other(k)}, device_id_type=MESH)
    own_c.wait()
    own_f.wait()
    pl.semaphore_wait(barrier, 2 + nf - 1)

    for p in (1, 2):
        c_move(p).start()
    for c in range(parts):
        for p in (1, 2):
            f_move(p, c).start()

    def c_phases(i, carry):
        at = pl.ds(pl.multiple_of(i * STEP, STEP), STEP)
        lag = lax.broadcasted_iota(jnp.int32, (LC, STEP), 0) * CSTRIDE
        f = fx * cbins + i * STEP + lax.broadcasted_iota(jnp.int32, (LC, STEP), 1)
        cos, sin = unit_phase((f * lag * scale) & (PERIOD - 1))
        w = cw[:, at]
        ctab[0, :, at] = cos * w
        ctab[1, :, at] = sin * w
        return carry

    lax.fori_loop(0, cbins // STEP, c_phases, 0)

    def f_phases(i, carry):
        at = pl.ds(pl.multiple_of(i * STEP, STEP), STEP)
        lag = lax.broadcasted_iota(jnp.int32, (LF, STEP), 0)
        f = fx * fbins + i * STEP + lax.broadcasted_iota(jnp.int32, (LF, STEP), 1)
        cos, sin = unit_phase((f * lag) & (PERIOD - 1))
        w = fw[:, at]
        ftab[0, :, at] = cos * w
        ftab[1, :, at] = sin * w
        return carry

    lax.fori_loop(0, fbins // STEP, f_phases, 0)

    rows = lax.broadcasted_iota(jnp.int32, (16, 8 * segs), 0)
    cols = lax.broadcasted_iota(jnp.int32, (16, 8 * segs), 1)
    orow = lax.broadcasted_iota(jnp.int32, (8, LANES), 0)
    for g in range(groups):
        pick = jnp.zeros((16, 8 * segs), jnp.float32)
        shift = jnp.zeros((8, LANES), jnp.int32)
        for i in range(4):
            base = source(4 * g + i) * segs
            found = jnp.int32(0)
            for s in range(segs):
                for k in range(2):
                    hit = jnp.where(trig[base + s, k] == me, 1, 0)
                    slot = 2 * i + found
                    col = (i * segs + s) * 2
                    here = ((rows == slot) & (cols == col)) | ((rows == 8 + slot) & (cols == col + 1))
                    pick += jnp.where(here, hit.astype(jnp.float32), 0.0)
                    shift += jnp.where(orow == slot, hit * offs[base + s, k], 0)
                    found = found + hit
        sel[g] = pick.astype(jnp.bfloat16)
        soff[g] = shift

    load_ct.wait()

    def c_power(i, total):
        at = pl.ds(pl.multiple_of(i * LANES, LANES), LANES)
        re = ct[:ctn, at].astype(jnp.float32)
        im = ct[ctn:, at].astype(jnp.float32)
        return total + (re * re + im * im) * cw[:, at]

    ct_sum = lax.fori_loop(0, cbins // LANES, c_power, jnp.zeros((ctn, LANES), jnp.float32))
    ct_sum = jnp.broadcast_to(jnp.sum(ct_sum, axis=1, keepdims=True), (ctn, LANES))
    load_ft.wait()

    def f_power(i, total):
        at = pl.ds(pl.multiple_of(i * LANES, LANES), LANES)
        re = ft[:ftn, at].astype(jnp.float32)
        im = ft[ftn:, at].astype(jnp.float32)
        return total + (re * re + im * im) * fw[:, at]

    ft_sum = lax.fori_loop(0, fbins // LANES, f_power, jnp.zeros((ftn, LANES), jnp.float32))
    ft_sum = jnp.broadcast_to(jnp.sum(ft_sum, axis=1, keepdims=True), (ftn, LANES))
    for q in range(nf):
        nstage[q, :cq] = ct_sum[q * cq : (q + 1) * cq]
        nstage[q, cq:] = ft_sum[q * fq : (q + 1) * fq]

    def coarse_group(g):
        prow = lax.broadcasted_iota(jnp.int32, (8 * segs, 8 * segs), 0)
        pcol = lax.broadcasted_iota(jnp.int32, (8 * segs, 8 * segs), 1)
        half = 4 * segs
        want = jnp.where(prow < half, 2 * prow, 2 * (prow - half) + 1)
        split = jnp.where(pcol == want, 1.0, 0.0).astype(jnp.bfloat16)
        cpq[...] = jnp.zeros_like(cpq)
        ncol = LC * half

        def step(i, carry):
            at = pl.ds(pl.multiple_of(i * STEP, STEP), STEP)
            block = jnp.concatenate([cbuf[4 * g + b, :, at].astype(jnp.float32) for b in range(4)], axis=0)
            y = lax.dot_general(split, block.astype(jnp.bfloat16), NN, preferred_element_type=jnp.float32)
            yr, yi = y[:half], y[half:]
            for j in range(LC):
                c = ctab[0, j : j + 1, at]
                s = ctab[1, j : j + 1, at]
                clag[j * half : (j + 1) * half] = (yr * c - yi * s).astype(jnp.bfloat16)
                clag[ncol + j * half : ncol + (j + 1) * half] = (yr * s + yi * c).astype(jnp.bfloat16)
            cpq[...] += lax.dot_general(ct[:, at], clag[...], NT, preferred_element_type=jnp.float32)
            return carry

        lax.fori_loop(0, cbins // STEP, step, 0)
        re = cpq[:ctn, :ncol] + cpq[ctn:, ncol:]
        im = cpq[:ctn, ncol:] - cpq[ctn:, :ncol]
        for q in range(nf):
            cstage[g, q, :cq] = re[q * cq : (q + 1) * cq]
            cstage[g, q, cq:] = im[q * cq : (q + 1) * cq]

    def fine_piece(g, c):
        ncol = LF * 8
        if c == 0:
            fpq[...] = jnp.zeros_like(fpq)

        def step(i, carry):
            begin = c * fpart + i * STEP
            at = pl.ds(pl.multiple_of(begin, STEP), STEP)
            block = jnp.concatenate([fbuf[4 * g + b, :, at].astype(jnp.float32) for b in range(4)], axis=0)
            y = lax.dot_general(sel[g], block.astype(jnp.bfloat16), NN, preferred_element_type=jnp.float32)
            yr, yi = y[:8], y[8:]
            f = fx * fbins + begin + lax.broadcasted_iota(jnp.int32, (8, STEP), 1)
            cos, sin = unit_phase((f * soff[g, :, 0:1]) & (PERIOD - 1))
            sr = yr * cos - yi * sin
            si = yr * sin + yi * cos
            for j in range(0, LF, 2):
                res, ims = [], []
                for jj in (j, j + 1):
                    wc = ftab[0, jj : jj + 1, at]
                    ws = ftab[1, jj : jj + 1, at]
                    res.append(sr * wc - si * ws)
                    ims.append(sr * ws + si * wc)
                flag[j * 8 : j * 8 + 16] = jnp.concatenate(res, axis=0).astype(jnp.bfloat16)
                flag[ncol + j * 8 : ncol + j * 8 + 16] = jnp.concatenate(ims, axis=0).astype(jnp.bfloat16)
            fpq[...] += lax.dot_general(ft[:, at], flag[...], NT, preferred_element_type=jnp.float32)
            return carry

        lax.fori_loop(0, fpart // STEP, step, 0)
        if c == parts - 1:
            re = fpq[:ftn, :ncol] + fpq[ftn:, ncol:]
            im = fpq[:ftn, ncol:] - fpq[ftn:, :ncol]
            for q in range(nf):
                fstage[g, q, :fq] = re[q * fq : (q + 1) * fq]
                fstage[g, q, fq:] = im[q * fq : (q + 1) * fq]

    def coarse_peak(g):
        total = cstage[g, fx]
        for k in range(1, nf):
            cx_move(g, k).wait_recv()
            total = total + crecv[g, k - 1]
        energy = total[:cq] * total[:cq] + total[cq:] * total[cq:]
        half = 4 * segs
        peak = energy[:, :LANES]
        for b in range(1, LC * half // LANES):
            peak = jnp.maximum(peak, energy[:, b * LANES : (b + 1) * LANES])
        span = LANES // 2
        while span >= half:
            peak = jnp.maximum(peak, pltpu.roll(peak, span, 1))
            span //= 2
        peak = peak / cnorm[...]
        lane = lax.broadcasted_iota(jnp.int32, (cq, LANES), 1) // segs
        for i in range(4):
            src = source(4 * g + i)
            moved = pltpu.roll(peak, lax.rem(src * segs + LANES - i * segs, LANES), 1)
            cres[...] = jnp.where(lane == src, moved, cres[...])

    def fine_peak(g):
        total = fstage[g, fx]
        for k in range(1, nf):
            fx_move(g, k).wait_recv()
            total = total + frecv[g, k - 1]
        energy = total[:fq] * total[:fq] + total[fq:] * total[fq:]
        peak = energy
        span = LANES // 2
        while span >= 8:
            peak = jnp.maximum(peak, pltpu.roll(peak, span, 1))
            span //= 2
        peak = peak / fnorm[...]
        square = jnp.concatenate([peak, jnp.zeros((LANES - fq, LANES), jnp.float32)], axis=0)
        rstage[g] = square.T[:8]

    def norms():
        total = nstage[fx]
        for k in range(1, nf):
            n_move(k).wait_recv()
            total = total + nrecv[k - 1]
        cnorm[...] = total[:cq]
        fnorm[...] = total[cq:]
        cres[...] = jnp.zeros_like(cres)

    def give_back(g):
        for p in range(4 * g, 4 * g + 4):
            if p > 0:
                r_move(p).start()

    for g in range(groups):
        for h in (2 * g + 1, 2 * g + 2):
            second = h == 2 * g + 2
            here = [p for p in (2 * h - 1, 2 * h) if p <= nb - 1]
            for p in here:
                c_move(p).wait_recv()
                if p + 2 <= nb - 1:
                    c_move(p + 2).start()
            if second:
                coarse_group(g)
            order = list(range(parts))
            if here == [nb - 1]:
                order = [c for pair in zip(order[: parts // 2], order[parts // 2 :]) for c in pair]
            for c in order:
                for p in here:
                    f_move(p, c).wait_recv()
                    if p + 2 <= nb - 1 and not (p + 2 == nb - 1 and c >= parts // 2):
                        f_move(p + 2, c).start()
                    if p + 1 == nb - 1 and c >= parts // 2:
                        f_move(p + 1, c).start()
                if second:
                    fine_piece(g, c)
                    if c == 0:
                        for k in range(1, nf):
                            cx_move(g, k).start()
                elif g == 0 and c == 0:
                    for k in range(1, nf):
                        n_move(k).start()
            if not second and g == 0:
                norms()
            if not second and g > 0:
                coarse_peak(g - 1)
                fine_peak(g - 1)
                give_back(g - 1)
        for k in range(1, nf):
            fx_move(g, k).start()
    coarse_peak(groups - 1)
    fine_peak(groups - 1)
    give_back(groups - 1)
    coarse_out[...] = cres[...]
    rrecv[0] = rstage[0]
    for p in range(1, nb):
        r_move(p).wait_recv()

    result = jnp.zeros((8, LANES), jnp.float32)
    named = []
    for s in range(segs):
        for k in range(2):
            bank = trig[me * segs + s, k]
            rank = jnp.int32(0)
            for before in named:
                rank = rank + jnp.where(before == bank, 1, 0)
            named.append(bank)
            away = lax.rem(me - bank + nb, nb)
            place = jnp.where(away < nb // 2, 2 * away, 2 * (nb - away) - 1)
            row = lax.rem(place, 4) * 2 + rank
            tile = rrecv[place]
            line = jnp.sum(jnp.where(orow == row, tile, 0.0), axis=0, keepdims=True)
            result = jnp.where(orow == 2 * s + k, line, result)
    fine_out[...] = result

    for p in range(1, nb):
        c_move(p).wait_send()
        for c in range(parts):
            f_move(p, c).wait_send()
        r_move(p).wait_send()
    for k in range(1, nf):
        n_move(k).wait_send()
        for g in range(groups):
            cx_move(g, k).wait_send()
            fx_move(g, k).wait_send()


def body(
    nb,
    nf,
    coarse_spectra,
    fine_spectra,
    coarse_templates,
    fine_templates,
    coarse_weight,
    fine_weight,
    triggers,
    offsets,
):
    segs, _, cbins = coarse_spectra.shape
    fbins = fine_spectra.shape[2]
    ctn = coarse_templates.shape[1]
    ftn = fine_templates.shape[2]
    groups = nb // 4
    parts = 4
    cq, fq = ctn // nf, ftn // nf
    ccol, fcol = LC * 4 * segs, LF * 8
    f32, bf16 = jnp.float32, jnp.bfloat16
    dma = pltpu.SemaphoreType.DMA
    anywhere = pl.BlockSpec(memory_space=pl.ANY)
    smem = pl.BlockSpec(memory_space=pltpu.SMEM)
    vmem = pl.BlockSpec(memory_space=pltpu.VMEM)
    coarse, fine = pl.pallas_call(
        functools.partial(kernel, nb, nf),
        out_shape=(
            jax.ShapeDtypeStruct((cq, LANES), f32),
            jax.ShapeDtypeStruct((8, LANES), f32),
        ),
        in_specs=[smem, smem, anywhere, anywhere, anywhere, anywhere, vmem, vmem],
        out_specs=(vmem, vmem),
        scratch_shapes=[
            pltpu.VMEM((nb, 2 * segs, cbins), bf16),
            pltpu.VMEM((nb, 2 * segs, fbins), bf16),
            pltpu.VMEM((2 * ctn, cbins), bf16),
            pltpu.VMEM((2 * ftn, fbins), bf16),
            pltpu.VMEM((2, LC, cbins), f32),
            pltpu.VMEM((2, LF, fbins), f32),
            pltpu.VMEM((2 * ccol, STEP), bf16),
            pltpu.VMEM((2 * fcol, STEP), bf16),
            pltpu.VMEM((2 * ctn, 2 * ccol), f32),
            pltpu.VMEM((2 * ftn, 2 * fcol), f32),
            pltpu.VMEM((groups, 16, 8 * segs), bf16),
            pltpu.VMEM((groups, 8, LANES), jnp.int32),
            pltpu.VMEM((groups, nf, 2 * cq, ccol), f32),
            pltpu.VMEM((groups, nf - 1, 2 * cq, ccol), f32),
            pltpu.VMEM((groups, nf, 2 * fq, fcol), f32),
            pltpu.VMEM((groups, nf - 1, 2 * fq, fcol), f32),
            pltpu.VMEM((nf, cq + fq, LANES), f32),
            pltpu.VMEM((nf - 1, cq + fq, LANES), f32),
            pltpu.VMEM((cq, LANES), f32),
            pltpu.VMEM((fq, LANES), f32),
            pltpu.VMEM((cq, LANES), f32),
            pltpu.VMEM((groups, 8, LANES), f32),
            pltpu.VMEM((nb, 8, LANES), f32),
            dma((2,)),
            dma,
            dma,
            dma((nb,)),
            dma((nb,)),
            dma((nb, parts)),
            dma((nb, parts)),
            dma((nf - 1,)),
            dma((nf - 1,)),
            dma((groups, nf - 1)),
            dma((groups, nf - 1)),
            dma((groups, nf - 1)),
            dma((groups, nf - 1)),
            dma((nb,)),
            dma((nb,)),
        ],
        compiler_params=pltpu.CompilerParams(
            collective_id=0, has_side_effects=True, vmem_limit_bytes=48 * 1024 * 1024
        ),
        name="search",
    )(
        triggers,
        offsets,
        coarse_spectra.reshape(2 * segs, cbins),
        fine_spectra.reshape(2 * segs, fbins),
        coarse_templates.reshape(2 * ctn, cbins),
        fine_templates.reshape(2 * ftn, fbins),
        coarse_weight.reshape(1, cbins),
        fine_weight.reshape(1, fbins),
    )
    coarse_snr = coarse[:, : nb * segs]
    fine_snr = fine[:, :fq].reshape(segs, 2, fq)
    return coarse_snr, fine_snr


def solution(mesh):
    return jax.shard_map(
        functools.partial(body, mesh.shape["bank"], mesh.shape["freq"]),
        mesh=mesh,
        in_specs=(
            P(("groups", "seg", "bank"), None, "freq"),
            P(("groups", "seg", "bank"), None, "freq"),
            P(None, "bank", "freq"),
            P(None, "bank", None, "freq"),
            P(("groups", "freq")),
            P(("groups", "freq")),
            P(("groups", "seg"), None),
            P(("groups", "seg"), None),
        ),
        out_specs=(
            P(("bank", "freq"), ("groups", "seg")),
            P(("groups", "seg", "bank"), None, "freq"),
        ),
        check_vma=False,
    )
```

time: 318 us -> 131 us (0.41); the launches traced: 313 us -> 131 us
  Pallas kernels: 0 us -> 123 us
  other arithmetic: 83.4 us -> 0 us
  waiting for transfers between devices: 74.2 us -> 0 us
  starting transfers between devices: 52.1 us -> 0 us
  matrix products: 40.5 us -> 0 us
  local copies, waits for them, and re-layouts: 47.1 us -> 7.8 us
  between operations: 14.9 us -> 0.65 us
    pallas_call x0 -> x1, Pallas kernels: none -> 123 us  [body(): pl.pallas_call(functools.partial(kernel, nb, nf), out_shape=(jax.ShapeDty...]
    all_to_all x6 -> x0, waiting for transfers between devices: 73.5 us -> none  [the longest x1 44.7 us: copy_for_each(): lax.all_to_all(jnp.broadcast_to(x[None], (size, *x.shape)), axis, 0, 0, t...]
    all_to_all x6 -> x0, starting transfers between devices: 52 us -> none  [the longest x5 27.9 us: sent_and_summed(): lax.all_to_all(blocks, axis, split_axis=0, concat_axis=0, tiled=True)]
    dot_general x38 -> x0, matrix products: 40.5 us -> none  [the longest x9 9.24 us: correlate(): jnp.dot(temp_imag, lag_imag, preferred_element_type=jnp.float32)]
    cos x9 -> x0, other arithmetic: 34.3 us -> none  [phase_of(): return (jnp.cos(radians), jnp.sin(radians))]
    transpose x9 -> x0, other arithmetic: 23.1 us -> none  [the longest x8 22 us: lagged(): left_real = real_part.T[:, :, None]]
    convert_element_type x11 -> x0, other arithmetic: 14.7 us -> none  [the longest x9 14.1 us: lagged(): (left_real * right_cos - left_imag * right_sin).astype(jnp.bfloat16)]
    dynamic_slice x8 -> x0, local copies, waits for them, and re-layouts: 9.1 us -> none  [body(): pieces = lax.map(run_group, (grouped, grouped_offsets))]
  transfers between devices with their start and end apart: 7 -> 0, of which waited for: 5 -> 0; matrix products, arithmetic and copies ran while one was open for 13% -> 0% of each run, Pallas kernels for 0% -> 0%
where the time goes in v1:
time: 131 us
  Pallas kernels  123 us (94%)
  local copies, waits for them, and re-layouts  7.8 us (6%)
    pallas_call x1, Pallas kernels, body(): pl.pallas_call(functools.partial(kernel, nb, nf), out_shape=(jax.ShapeDty...  123 us
    unnamed x10, local copies, waits for them, and re-layouts  5.88 us

profile of v1, /device:TPU:40, one launch (start us, length us, event | category | flops | bytes accessed | tf_op | source)
XLA Modules:
  0.0 131.1 jit_solution(9541278320134166787)
XLA Ops:
  0.6 0.8 copy.10.trig
  1.4 0.8 copy.11.offs
  2.2 0.9 reshape.25.cs_hbm
  3.0 1.1 reshape.26.fs_hbm
  4.1 0.0 copy-start
  4.1 1.6 %copy-done = bf16[2,128,4096]{2,1,0:T(8,128)(2,1)S(1)} copy-done((bf16[2,128,4096]{2,1,0:T(8,128)(2,1)S(1)}, bf16[2,128,4096]{2,1,0:T(8,128)(2,1)}, u32[]{:S(2)}) %copy-start) | copy-done | bytes 2097176
  5.7 0.0 copy-start.1
  5.7 0.8 copy-done.1
  6.5 0.0 copy-start.2
  6.5 0.7 copy-done.2
  7.2 122.7 %search.1 = (f32[32,128]{1,0:T(8,128)S(1)}, f32[8,128]{1,0:T(8,128)S(1)}) custom-call(s32[64,2]{1,0:T(8,128)S(1)} %copy.10.trig, s32[64,2]{1,0:T(8,128)S(1)} %copy.11.offs, bf16[8,4096]{1,0:T(8,128)(2,1)S(1)} %reshape.25.cs_hbm, bf16[8,16384]{1,0:T(8,128)(2,1)S(1)} %reshape.26.fs_hbm, bf16[256,4096]{1,0:T(8,128)(2,1)S(1)} %bitcast.7, ...), custom_call_target="tpu_custom_call" | custom-call | tf_op jit(solution)/shard_map/search/pallas_call | solution.py:484
  129.9 0.6 copy.14
  130.5 0.6 copy.15
Async XLA Ops:
  4.1 1.6 %copy-start = (bf16[2,128,4096]{2,1,0:T(8,128)(2,1)S(1)}, bf16[2,128,4096]{2,1,0:T(8,128)(2,1)}, u32[]{:S(2)}) copy-start(bf16[2,128,4096]{2,1,0:T(8,128)(2,1)} %param.10) | copy-start | bytes 6291460
  5.7 0.8 copy-start.1
  6.5 0.7 copy-start.2

commit v2 on v1

--- a/solution.py
+++ b/solution.py
@@ -16,6 +16,7 @@
 CSTRIDE = 2047
 PERIOD = 131072
 STEP = 512
+DEEP = 2048
 LANES = 128
 MESH = pl.DeviceIdType.MESH
 NT = (((1,), (1,)), ((), ()))
@@ -45,14 +46,20 @@
     fs_hbm,
     ct_hbm,
     ft_hbm,
-    cw,
-    fw,
+    cw_hbm,
+    fw_hbm,
     coarse_out,
     fine_out,
+    craw,
+    fraw,
     cbuf,
     fbuf,
     ct,
     ft,
+    cw,
+    fw,
+    cpure,
+    fpure,
     ctab,
     ftab,
     clag,
@@ -73,6 +80,7 @@
     rstage,
     rrecv,
     load_sem,
+    w_sem,
     ct_sem,
     ft_sem,
     c_send,
@@ -124,9 +132,9 @@
 
     def f_move(p, c):
         last = p == nb - 1
-        leftward = p % 2 == 0 or (last and c >= parts // 2)
+        leftward = p % 2 == 0 or (last and not isinstance(c, jax.Array) and c >= parts // 2)
         origin = p - 1 if (last and leftward) else max(p - 2, 0)
-        part = pl.ds(c * fpart, fpart)
+        part = pl.ds(pl.multiple_of(c * fpart, fpart), fpart)
         return pltpu.make_async_remote_copy(
             src_ref=fbuf.at[origin, :, part],
             dst_ref=fbuf.at[p, :, part],
@@ -176,10 +184,14 @@
             device_id_type=MESH,
         )
 
-    own_c = pltpu.make_async_copy(cs_hbm, cbuf.at[0], load_sem.at[0])
-    own_f = pltpu.make_async_copy(fs_hbm, fbuf.at[0], load_sem.at[1])
+    own_c = pltpu.make_async_copy(cs_hbm, craw, load_sem.at[0])
+    own_f = pltpu.make_async_copy(fs_hbm, fraw, load_sem.at[1])
     own_c.start()
     own_f.start()
+    load_cw = pltpu.make_async_copy(cw_hbm, cw, w_sem.at[0])
+    load_fw = pltpu.make_async_copy(fw_hbm, fw, w_sem.at[1])
+    load_cw.start()
+    load_fw.start()
     load_ct = pltpu.make_async_copy(ct_hbm, ct, ct_sem)
     load_ft = pltpu.make_async_copy(ft_hbm, ft, ft_sem)
     load_ct.start()
@@ -192,13 +204,24 @@
         pl.semaphore_signal(barrier, inc=1, device_id={"freq": other(k)}, device_id_type=MESH)
     own_c.wait()
     own_f.wait()
+
+    def settle(raw, buf, begin, size):
+        for at in range(begin, begin + size, STEP):
+            piece = [raw[r, :, at : at + STEP].astype(jnp.float32) for r in range(segs)]
+            buf[0, :, at : at + STEP] = jnp.concatenate(piece, axis=0).astype(jnp.bfloat16)
+
+    settle(craw, cbuf, 0, cbins)
+    settle(fraw, fbuf, 0, fpart)
     pl.semaphore_wait(barrier, 2 + nf - 1)
-
     for p in (1, 2):
         c_move(p).start()
     for c in range(parts):
+        if c + 1 < parts:
+            settle(fraw, fbuf, (c + 1) * fpart, fpart)
         for p in (1, 2):
             f_move(p, c).start()
+    load_cw.wait()
+    load_fw.wait()
 
     def c_phases(i, carry):
         at = pl.ds(pl.multiple_of(i * STEP, STEP), STEP)
@@ -235,103 +258,122 @@
             found = jnp.int32(0)
             for s in range(segs):
                 for k in range(2):
-                    hit = jnp.where(trig[base + s, k] == me, 1, 0)
+                    hit = jnp.where(trig[k, base + s] == me, 1, 0)
                     slot = 2 * i + found
                     col = (i * segs + s) * 2
                     here = ((rows == slot) & (cols == col)) | ((rows == 8 + slot) & (cols == col + 1))
                     pick += jnp.where(here, hit.astype(jnp.float32), 0.0)
-                    shift += jnp.where(orow == slot, hit * offs[base + s, k], 0)
+                    shift += jnp.where(orow == slot, hit * offs[k, base + s], 0)
                     found = found + hit
         sel[g] = pick.astype(jnp.bfloat16)
         soff[g] = shift
 
-    load_ct.wait()
-
-    def c_power(i, total):
-        at = pl.ds(pl.multiple_of(i * LANES, LANES), LANES)
-        re = ct[:ctn, at].astype(jnp.float32)
-        im = ct[ctn:, at].astype(jnp.float32)
-        return total + (re * re + im * im) * cw[:, at]
-
-    ct_sum = lax.fori_loop(0, cbins // LANES, c_power, jnp.zeros((ctn, LANES), jnp.float32))
-    ct_sum = jnp.broadcast_to(jnp.sum(ct_sum, axis=1, keepdims=True), (ctn, LANES))
-    load_ft.wait()
-
-    def f_power(i, total):
-        at = pl.ds(pl.multiple_of(i * LANES, LANES), LANES)
-        re = ft[:ftn, at].astype(jnp.float32)
-        im = ft[ftn:, at].astype(jnp.float32)
-        return total + (re * re + im * im) * fw[:, at]
-
-    ft_sum = lax.fori_loop(0, fbins // LANES, f_power, jnp.zeros((ftn, LANES), jnp.float32))
-    ft_sum = jnp.broadcast_to(jnp.sum(ft_sum, axis=1, keepdims=True), (ftn, LANES))
-    for q in range(nf):
-        nstage[q, :cq] = ct_sum[q * cq : (q + 1) * cq]
-        nstage[q, cq:] = ft_sum[q * fq : (q + 1) * fq]
+    def powers():
+        load_ct.wait()
+
+        def c_power(i, total):
+            at = pl.ds(pl.multiple_of(i * LANES, LANES), LANES)
+            re = ct[:ctn, at].astype(jnp.float32)
+            im = ct[ctn:, at].astype(jnp.float32)
+            return total + (re * re + im * im) * cw[:, at]
+
+        ct_sum = lax.fori_loop(0, cbins // LANES, c_power, jnp.zeros((ctn, LANES), jnp.float32))
+        ct_sum = jnp.broadcast_to(jnp.sum(ct_sum, axis=1, keepdims=True), (ctn, LANES))
+        load_ft.wait()
+
+        def f_power(i, total):
+            at = pl.ds(pl.multiple_of(i * LANES, LANES), LANES)
+            re = ft[:ftn, at].astype(jnp.float32)
+            im = ft[ftn:, at].astype(jnp.float32)
+            return total + (re * re + im * im) * fw[:, at]
+
+        ft_sum = lax.fori_loop(0, fbins // LANES, f_power, jnp.zeros((ftn, LANES), jnp.float32))
+        ft_sum = jnp.broadcast_to(jnp.sum(ft_sum, axis=1, keepdims=True), (ftn, LANES))
+        for q in range(nf):
+            nstage[q, :cq] = ct_sum[q * cq : (q + 1) * cq]
+            nstage[q, cq:] = ft_sum[q * fq : (q + 1) * fq]
 
     def coarse_group(g):
-        prow = lax.broadcasted_iota(jnp.int32, (8 * segs, 8 * segs), 0)
-        pcol = lax.broadcasted_iota(jnp.int32, (8 * segs, 8 * segs), 1)
         half = 4 * segs
+        prow = lax.broadcasted_iota(jnp.int32, (2 * half, 2 * half), 0)
+        pcol = lax.broadcasted_iota(jnp.int32, (2 * half, 2 * half), 1)
         want = jnp.where(prow < half, 2 * prow, 2 * (prow - half) + 1)
         split = jnp.where(pcol == want, 1.0, 0.0).astype(jnp.bfloat16)
+        ncol = LC * half
+        wide = min(2 * STEP, cbins)
+        for begin in range(0, cbins, wide):
+            at = slice(begin, begin + wide)
+            block = jnp.concatenate([cbuf[4 * g + b, :, at].astype(jnp.float32) for b in range(4)], axis=0)
+            cpure[:, at] = lax.dot_general(split, block.astype(jnp.bfloat16), NN, preferred_element_type=jnp.float32)
         cpq[...] = jnp.zeros_like(cpq)
-        ncol = LC * half
+        deep = min(DEEP, cbins)
 
         def step(i, carry):
-            at = pl.ds(pl.multiple_of(i * STEP, STEP), STEP)
-            block = jnp.concatenate([cbuf[4 * g + b, :, at].astype(jnp.float32) for b in range(4)], axis=0)
-            y = lax.dot_general(split, block.astype(jnp.bfloat16), NN, preferred_element_type=jnp.float32)
-            yr, yi = y[:half], y[half:]
-            for j in range(LC):
-                c = ctab[0, j : j + 1, at]
-                s = ctab[1, j : j + 1, at]
-                clag[j * half : (j + 1) * half] = (yr * c - yi * s).astype(jnp.bfloat16)
-                clag[ncol + j * half : ncol + (j + 1) * half] = (yr * s + yi * c).astype(jnp.bfloat16)
-            cpq[...] += lax.dot_general(ct[:, at], clag[...], NT, preferred_element_type=jnp.float32)
+            base = pl.multiple_of(i * deep, deep)
+            for kt in range(0, deep, 2 * LANES):
+                at = pl.ds(base + kt, 2 * LANES)
+                yr, yi = cpure[:half, at], cpure[half:, at]
+                for j in range(LC):
+                    c = ctab[0, j : j + 1, at]
+                    s = ctab[1, j : j + 1, at]
+                    clag[j * half : (j + 1) * half, kt : kt + 2 * LANES] = (yr * c - yi * s).astype(jnp.bfloat16)
+                    clag[ncol + j * half : ncol + (j + 1) * half, kt : kt + 2 * LANES] = (yr * s + yi * c).astype(jnp.bfloat16)
+            cpq[...] += lax.dot_general(clag[...], ct[:, pl.ds(base, deep)], NT, preferred_element_type=jnp.float32)
             return carry
 
-        lax.fori_loop(0, cbins // STEP, step, 0)
-        re = cpq[:ctn, :ncol] + cpq[ctn:, ncol:]
-        im = cpq[:ctn, ncol:] - cpq[ctn:, :ncol]
+        lax.fori_loop(0, cbins // deep, step, 0)
+        re = (cpq[:ncol, :ctn] + cpq[ncol:, ctn:]).T
+        im = (cpq[ncol:, :ctn] - cpq[:ncol, ctn:]).T
         for q in range(nf):
             cstage[g, q, :cq] = re[q * cq : (q + 1) * cq]
             cstage[g, q, cq:] = im[q * cq : (q + 1) * cq]
 
     def fine_piece(g, c):
         ncol = LF * 8
-        if c == 0:
-            fpq[...] = jnp.zeros_like(fpq)
-
-        def step(i, carry):
-            begin = c * fpart + i * STEP
-            at = pl.ds(pl.multiple_of(begin, STEP), STEP)
+        wide = min(2 * STEP, fpart)
+        for begin in range(0, fpart, wide):
+            first = c * fpart + begin
+            at = pl.ds(pl.multiple_of(first, wide), wide)
             block = jnp.concatenate([fbuf[4 * g + b, :, at].astype(jnp.float32) for b in range(4)], axis=0)
             y = lax.dot_general(sel[g], block.astype(jnp.bfloat16), NN, preferred_element_type=jnp.float32)
+            f = fx * fbins + first + lax.broadcasted_iota(jnp.int32, (8, wide), 1)
+            shift = jnp.concatenate([soff[g]] * (wide // LANES), axis=1)
+            cos, sin = unit_phase((f * shift) & (PERIOD - 1))
             yr, yi = y[:8], y[8:]
-            f = fx * fbins + begin + lax.broadcasted_iota(jnp.int32, (8, STEP), 1)
-            cos, sin = unit_phase((f * soff[g, :, 0:1]) & (PERIOD - 1))
-            sr = yr * cos - yi * sin
-            si = yr * sin + yi * cos
-            for j in range(0, LF, 2):
-                res, ims = [], []
-                for jj in (j, j + 1):
-                    wc = ftab[0, jj : jj + 1, at]
-                    ws = ftab[1, jj : jj + 1, at]
-                    res.append(sr * wc - si * ws)
-                    ims.append(sr * ws + si * wc)
-                flag[j * 8 : j * 8 + 16] = jnp.concatenate(res, axis=0).astype(jnp.bfloat16)
-                flag[ncol + j * 8 : ncol + j * 8 + 16] = jnp.concatenate(ims, axis=0).astype(jnp.bfloat16)
-            fpq[...] += lax.dot_general(ft[:, at], flag[...], NT, preferred_element_type=jnp.float32)
+            fpure[:8, begin : begin + wide] = yr * cos - yi * sin
+            fpure[8:, begin : begin + wide] = yr * sin + yi * cos
+        deep = min(DEEP, fpart)
+
+        def step(i, carry):
+            base = pl.multiple_of(i * deep, deep)
+            whole = pl.multiple_of(c * fpart + i * deep, deep)
+            for kt in range(0, deep, 2 * LANES):
+                sr = fpure[:8, pl.ds(base + kt, 2 * LANES)]
+                si = fpure[8:, pl.ds(base + kt, 2 * LANES)]
+                at = pl.ds(whole + kt, 2 * LANES)
+                for j in range(0, LF, 2):
+                    res, ims = [], []
+                    for jj in (j, j + 1):
+                        wc = ftab[0, jj : jj + 1, at]
+                        ws = ftab[1, jj : jj + 1, at]
+                        res.append(sr * wc - si * ws)
+                        ims.append(sr * ws + si * wc)
+                    here = slice(kt, kt + 2 * LANES)
+                    flag[j * 8 : j * 8 + 16, here] = jnp.concatenate(res, axis=0).astype(jnp.bfloat16)
+                    flag[ncol + j * 8 : ncol + j * 8 + 16, here] = jnp.concatenate(ims, axis=0).astype(jnp.bfloat16)
+            fpq[...] += lax.dot_general(flag[...], ft[:, pl.ds(whole, deep)], NT, preferred_element_type=jnp.float32)
             return carry
 
-        lax.fori_loop(0, fpart // STEP, step, 0)
-        if c == parts - 1:
-            re = fpq[:ftn, :ncol] + fpq[ftn:, ncol:]
-            im = fpq[:ftn, ncol:] - fpq[ftn:, :ncol]
-            for q in range(nf):
-                fstage[g, q, :fq] = re[q * fq : (q + 1) * fq]
-                fstage[g, q, fq:] = im[q * fq : (q + 1) * fq]
+        lax.fori_loop(0, fpart // deep, step, 0)
+
+    def fine_done(g):
+        ncol = LF * 8
+        top, bottom = fpq[:ncol], fpq[ncol:]
+        re = (top + pltpu.roll(bottom, ftn, 1)).T
+        im = (bottom - pltpu.roll(top, ftn, 1)).T
+        for q in range(nf):
+            fstage[g, q, :fq] = re[q * fq : (q + 1) * fq]
+            fstage[g, q, fq:] = im[q * fq : (q + 1) * fq]
 
     def coarse_peak(g):
         total = cstage[g, fx]
@@ -384,41 +426,59 @@
                 r_move(p).start()
 
     for g in range(groups):
-        for h in (2 * g + 1, 2 * g + 2):
-            second = h == 2 * g + 2
-            here = [p for p in (2 * h - 1, 2 * h) if p <= nb - 1]
+        here = (4 * g + 1, 4 * g + 2)
+        for p in here:
+            c_move(p).wait_recv()
+            if p + 2 <= nb - 1:
+                c_move(p + 2).start()
+        for c in range(parts):
             for p in here:
-                c_move(p).wait_recv()
-                if p + 2 <= nb - 1:
-                    c_move(p + 2).start()
-            if second:
-                coarse_group(g)
-            order = list(range(parts))
-            if here == [nb - 1]:
-                order = [c for pair in zip(order[: parts // 2], order[parts // 2 :]) for c in pair]
-            for c in order:
-                for p in here:
-                    f_move(p, c).wait_recv()
-                    if p + 2 <= nb - 1 and not (p + 2 == nb - 1 and c >= parts // 2):
-                        f_move(p + 2, c).start()
-                    if p + 1 == nb - 1 and c >= parts // 2:
-                        f_move(p + 1, c).start()
-                if second:
-                    fine_piece(g, c)
-                    if c == 0:
-                        for k in range(1, nf):
-                            cx_move(g, k).start()
-                elif g == 0 and c == 0:
+                f_move(p, c).wait_recv()
+                if p + 2 <= nb - 1 and not (p + 2 == nb - 1 and c >= parts // 2):
+                    f_move(p + 2, c).start()
+                if p + 1 == nb - 1 and c >= parts // 2:
+                    f_move(p + 1, c).start()
+        if g == 0:
+            powers()
+        else:
+            if g == 1:
+                norms()
+            coarse_peak(g - 1)
+            fine_peak(g - 1)
+            give_back(g - 1)
+        last = g == groups - 1
+        here = [p for p in (4 * g + 3, 4 * g + 4) if p <= nb - 1]
+        for p in here:
+            c_move(p).wait_recv()
+            if p + 2 <= nb - 1:
+                c_move(p + 2).start()
+        coarse_group(g)
+        fpq[...] = jnp.zeros_like(fpq)
+
+        def piece(i, carry, g=g, here=here, last=last):
+            c = (i % 2) * (parts // 2) + i // 2 if last else i
+            for p in here:
+                f_move(p, c).wait_recv()
+                if not last:
+                    f_move(p + 2, c).start()
+            fine_piece(g, c)
+
+            @pl.when(i == 0)
+            def _():
+                for k in range(1, nf):
+                    cx_move(g, k).start()
+                if g == 0:
                     for k in range(1, nf):
                         n_move(k).start()
-            if not second and g == 0:
-                norms()
-            if not second and g > 0:
-                coarse_peak(g - 1)
-                fine_peak(g - 1)
-                give_back(g - 1)
+
+            return carry
+
+        lax.fori_loop(0, parts, piece, 0)
+        fine_done(g)
         for k in range(1, nf):
             fx_move(g, k).start()
+    if groups == 1:
+        norms()
     coarse_peak(groups - 1)
     fine_peak(groups - 1)
     give_back(groups - 1)
@@ -431,7 +491,7 @@
     named = []
     for s in range(segs):
         for k in range(2):
-            bank = trig[me * segs + s, k]
+            bank = trig[k, me * segs + s]
             rank = jnp.int32(0)
             for before in named:
                 rank = rank + jnp.where(before == bank, 1, 0)
@@ -487,19 +547,25 @@
             jax.ShapeDtypeStruct((cq, LANES), f32),
             jax.ShapeDtypeStruct((8, LANES), f32),
         ),
-        in_specs=[smem, smem, anywhere, anywhere, anywhere, anywhere, vmem, vmem],
+        in_specs=[smem, smem] + [anywhere] * 6,
         out_specs=(vmem, vmem),
         scratch_shapes=[
+            pltpu.VMEM((segs, 2, cbins), bf16),
+            pltpu.VMEM((segs, 2, fbins), bf16),
             pltpu.VMEM((nb, 2 * segs, cbins), bf16),
             pltpu.VMEM((nb, 2 * segs, fbins), bf16),
             pltpu.VMEM((2 * ctn, cbins), bf16),
             pltpu.VMEM((2 * ftn, fbins), bf16),
+            pltpu.VMEM((1, cbins), f32),
+            pltpu.VMEM((1, fbins), f32),
+            pltpu.VMEM((8 * segs, cbins), f32),
+            pltpu.VMEM((16, fbins // parts), f32),
             pltpu.VMEM((2, LC, cbins), f32),
             pltpu.VMEM((2, LF, fbins), f32),
-            pltpu.VMEM((2 * ccol, STEP), bf16),
-            pltpu.VMEM((2 * fcol, STEP), bf16),
-            pltpu.VMEM((2 * ctn, 2 * ccol), f32),
-            pltpu.VMEM((2 * ftn, 2 * fcol), f32),
+            pltpu.VMEM((2 * ccol, min(DEEP, cbins)), bf16),
+            pltpu.VMEM((2 * fcol, min(DEEP, fbins // parts)), bf16),
+            pltpu.VMEM((2 * ccol, 2 * ctn), f32),
+            pltpu.VMEM((2 * fcol, 2 * ftn), f32),
             pltpu.VMEM((groups, 16, 8 * segs), bf16),
             pltpu.VMEM((groups, 8, LANES), jnp.int32),
             pltpu.VMEM((groups, nf, 2 * cq, ccol), f32),
@@ -513,6 +579,7 @@
             pltpu.VMEM((cq, LANES), f32),
             pltpu.VMEM((groups, 8, LANES), f32),
             pltpu.VMEM((nb, 8, LANES), f32),
+            dma((2,)),
             dma((2,)),
             dma,
             dma,
@@ -530,14 +597,14 @@
             dma((nb,)),
         ],
         compiler_params=pltpu.CompilerParams(
-            collective_id=0, has_side_effects=True, vmem_limit_bytes=48 * 1024 * 1024
+            collective_id=0, has_side_effects=True, vmem_limit_bytes=67043328
         ),
         name="search",
     )(
-        triggers,
-        offsets,
-        coarse_spectra.reshape(2 * segs, cbins),
-        fine_spectra.reshape(2 * segs, fbins),
+        triggers.T,
+        offsets.T,
+        coarse_spectra,
+        fine_spectra,
         coarse_templates.reshape(2 * ctn, cbins),
         fine_templates.reshape(2 * ftn, fbins),
         coarse_weight.reshape(1, cbins),

time: 131 us -> 98.7 us (0.75)
  Pallas kernels: 123 us -> 95.2 us
  local copies, waits for them, and re-layouts: 7.8 us -> 2.59 us
    pallas_call x1, Pallas kernels: 123 us -> 95.2 us  [body(): pl.pallas_call(functools.partial(kernel, nb, nf), out_shape=(jax.ShapeDty...]
    unnamed x10 -> x2, local copies, waits for them, and re-layouts: 5.88 us -> 2.59 us
    reshape x2 -> x0, local copies, waits for them, and re-layouts: 1.92 us -> none  [the longest x1 1.05 us: body(): fine_spectra.reshape(2 * segs, fbins)]
where the time goes in v2:
time: 98.7 us; the launch traced here: 98.4 us
  Pallas kernels  95.2 us (96%)
  local copies, waits for them, and re-layouts  2.59 us (3%)
    pallas_call x1, Pallas kernels, body(): pl.pallas_call(functools.partial(kernel, nb, nf), out_shape=(jax.ShapeDty...  95.2 us
    unnamed x2, local copies, waits for them, and re-layouts  2.59 us

profile of v2, /device:TPU:40, one launch (start us, length us, event | category | flops | bytes accessed | tf_op | source)
XLA Modules:
  0.0 98.4 jit_solution(16125734040171039697)
XLA Ops:
  0.6 95.2 %search.1 = (f32[32,128]{1,0:T(8,128)}, f32[8,128]{1,0:T(8,128)}) custom-call(s32[2,64]{1,0:T(2,128)} %bitcast.15, s32[2,64]{1,0:T(2,128)} %bitcast.16, bf16[4,2,4096]{2,1,0:T(2,128)(2,1)} %cs_hbm.1, bf16[4,2,16384]{2,1,0:T(2,128)(2,1)} %fs_hbm.1, bf16[256,4096]{1,0:T(8,128)(2,1)} %bitcast.10, bf16[128,16384]{1,0:T(8,128)(2,1)} %bitcast.9, ...), custom_call_target="tpu_custom_call" | custom-call | tf_op jit(solution)/shard_map/search/pallas_call | solution.py:544
  95.9 1.3 %copy.12 = f32[32,64]{1,0:T(8,128)} copy(f32[32,64]{1,0:T(8,128)} %bitcast.13) | data formatting | bytes 16384
  97.2 1.3 %copy.13 = f32[4,2,16]{2,1,0:T(2,128)} copy(f32[4,2,16]{2,1,0:T(2,128)} %bitcast.14) | data formatting | bytes 1024

commit v3 on v2

--- a/solution.py
+++ b/solution.py
@@ -58,6 +58,7 @@
     ft,
     cw,
     fw,
+    stab,
     cpure,
     fpure,
     ctab,
@@ -130,10 +131,10 @@
             device_id_type=MESH,
         )
 
-    def f_move(p, c):
-        last = p == nb - 1
-        leftward = p % 2 == 0 or (last and not isinstance(c, jax.Array) and c >= parts // 2)
-        origin = p - 1 if (last and leftward) else max(p - 2, 0)
+    def f_move(p, c, leftward=None):
+        if leftward is None:
+            leftward = p % 2 == 0
+        origin = p - 1 if (p == nb - 1 and leftward) else max(p - 2, 0)
         part = pl.ds(pl.multiple_of(c * fpart, fpart), fpart)
         return pltpu.make_async_remote_copy(
             src_ref=fbuf.at[origin, :, part],
@@ -176,7 +177,7 @@
 
     def r_move(p):
         return pltpu.make_async_remote_copy(
-            src_ref=rstage.at[p // 4],
+            src_ref=rstage.at[p // 4 if p < nb - 1 else groups],
             dst_ref=rrecv.at[p],
             send_sem=r_send.at[p],
             recv_sem=r_recv.at[p],
@@ -210,16 +211,17 @@
             piece = [raw[r, :, at : at + STEP].astype(jnp.float32) for r in range(segs)]
             buf[0, :, at : at + STEP] = jnp.concatenate(piece, axis=0).astype(jnp.bfloat16)
 
-    settle(craw, cbuf, 0, cbins)
     settle(fraw, fbuf, 0, fpart)
     pl.semaphore_wait(barrier, 2 + nf - 1)
-    for p in (1, 2):
-        c_move(p).start()
     for c in range(parts):
         if c + 1 < parts:
             settle(fraw, fbuf, (c + 1) * fpart, fpart)
+        else:
+            settle(craw, cbuf, 0, cbins)
         for p in (1, 2):
             f_move(p, c).start()
+    for p in (1, 2):
+        c_move(p).start()
     load_cw.wait()
     load_fw.wait()
 
@@ -247,26 +249,41 @@
 
     lax.fori_loop(0, fbins // STEP, f_phases, 0)
 
+    def single_phases():
+        def step(i, carry):
+            at = pl.ds(pl.multiple_of(i * STEP, STEP), STEP)
+            lag = lax.broadcasted_iota(jnp.int32, (2 * LF, STEP), 0) // 2
+            f = fx * fbins + i * STEP + lax.broadcasted_iota(jnp.int32, (2 * LF, STEP), 1)
+            cos, sin = unit_phase((f * lag) & (PERIOD - 1))
+            w = fw[:, at]
+            stab[0, :, at] = cos * w
+            stab[1, :, at] = sin * w
+            return carry
+
+        lax.fori_loop(0, fbins // STEP, step, 0)
+
     rows = lax.broadcasted_iota(jnp.int32, (16, 8 * segs), 0)
     cols = lax.broadcasted_iota(jnp.int32, (16, 8 * segs), 1)
     orow = lax.broadcasted_iota(jnp.int32, (8, LANES), 0)
-    for g in range(groups):
+    units = [list(range(4 * g, min(4 * g + 4, nb - 1))) for g in range(groups)] + [[nb - 1]]
+    for u, places in enumerate(units):
         pick = jnp.zeros((16, 8 * segs), jnp.float32)
         shift = jnp.zeros((8, LANES), jnp.int32)
-        for i in range(4):
-            base = source(4 * g + i) * segs
+        for i, p in enumerate(places):
+            base = source(p) * segs
             found = jnp.int32(0)
             for s in range(segs):
                 for k in range(2):
                     hit = jnp.where(trig[k, base + s] == me, 1, 0)
                     slot = 2 * i + found
+                    row = (rows & 7) & 1 if u == groups else rows & 7
                     col = (i * segs + s) * 2
-                    here = ((rows == slot) & (cols == col)) | ((rows == 8 + slot) & (cols == col + 1))
+                    here = (row == slot) & (cols == col + (rows >> 3))
                     pick += jnp.where(here, hit.astype(jnp.float32), 0.0)
-                    shift += jnp.where(orow == slot, hit * offs[k, base + s], 0)
+                    shift += jnp.where((orow & 1 if u == groups else orow) == slot, hit * offs[k, base + s], 0)
                     found = found + hit
-        sel[g] = pick.astype(jnp.bfloat16)
-        soff[g] = shift
+        sel[u] = pick.astype(jnp.bfloat16)
+        soff[u] = shift
 
     def powers():
         load_ct.wait()
@@ -328,16 +345,20 @@
             cstage[g, q, :cq] = re[q * cq : (q + 1) * cq]
             cstage[g, q, cq:] = im[q * cq : (q + 1) * cq]
 
-    def fine_piece(g, c):
-        ncol = LF * 8
+    def fine_piece(u, c):
+        single = u == groups
+        ncol = LF * (2 if single else 8)
+        table = stab if single else ftab
+        places = units[u] + (units[groups - 1] if single else [])
+        places = (places + places)[:4]
         wide = min(2 * STEP, fpart)
         for begin in range(0, fpart, wide):
             first = c * fpart + begin
             at = pl.ds(pl.multiple_of(first, wide), wide)
-            block = jnp.concatenate([fbuf[4 * g + b, :, at].astype(jnp.float32) for b in range(4)], axis=0)
-            y = lax.dot_general(sel[g], block.astype(jnp.bfloat16), NN, preferred_element_type=jnp.float32)
+            block = jnp.concatenate([fbuf[p, :, at].astype(jnp.float32) for p in places], axis=0)
+            y = lax.dot_general(sel[u], block.astype(jnp.bfloat16), NN, preferred_element_type=jnp.float32)
             f = fx * fbins + first + lax.broadcasted_iota(jnp.int32, (8, wide), 1)
-            shift = jnp.concatenate([soff[g]] * (wide // LANES), axis=1)
+            shift = jnp.concatenate([soff[u]] * (wide // LANES), axis=1)
             cos, sin = unit_phase((f * shift) & (PERIOD - 1))
             yr, yi = y[:8], y[8:]
             fpure[:8, begin : begin + wide] = yr * cos - yi * sin
@@ -351,29 +372,37 @@
                 sr = fpure[:8, pl.ds(base + kt, 2 * LANES)]
                 si = fpure[8:, pl.ds(base + kt, 2 * LANES)]
                 at = pl.ds(whole + kt, 2 * LANES)
-                for j in range(0, LF, 2):
+                here = slice(kt, kt + 2 * LANES)
+                for j in range(0, ncol // 8, 2):
                     res, ims = [], []
                     for jj in (j, j + 1):
-                        wc = ftab[0, jj : jj + 1, at]
-                        ws = ftab[1, jj : jj + 1, at]
+                        lag = slice(jj * 8, jj * 8 + 8) if single else slice(jj, jj + 1)
+                        wc = table[0, lag, at]
+                        ws = table[1, lag, at]
                         res.append(sr * wc - si * ws)
                         ims.append(sr * ws + si * wc)
-                    here = slice(kt, kt + 2 * LANES)
                     flag[j * 8 : j * 8 + 16, here] = jnp.concatenate(res, axis=0).astype(jnp.bfloat16)
                     flag[ncol + j * 8 : ncol + j * 8 + 16, here] = jnp.concatenate(ims, axis=0).astype(jnp.bfloat16)
-            fpq[...] += lax.dot_general(flag[...], ft[:, pl.ds(whole, deep)], NT, preferred_element_type=jnp.float32)
+            fpq[: 2 * ncol] += lax.dot_general(
+                flag[: 2 * ncol], ft[:, pl.ds(whole, deep)], NT, preferred_element_type=jnp.float32
+            )
             return carry
 
         lax.fori_loop(0, fpart // deep, step, 0)
 
-    def fine_done(g):
-        ncol = LF * 8
-        top, bottom = fpq[:ncol], fpq[ncol:]
-        re = (top + pltpu.roll(bottom, ftn, 1)).T
-        im = (bottom - pltpu.roll(top, ftn, 1)).T
+    def fine_done(u):
+        ncol = LF * (2 if u == groups else 8)
+        top, bottom = fpq[:ncol], fpq[ncol : 2 * ncol]
+        re = top + pltpu.roll(bottom, ftn, 1)
+        im = bottom - pltpu.roll(top, ftn, 1)
+        if ncol < LANES:
+            rest = jnp.zeros((LANES - ncol, LANES), jnp.float32)
+            re = jnp.concatenate([re, rest], axis=0)
+            im = jnp.concatenate([im, rest], axis=0)
+        re, im = re.T, im.T
         for q in range(nf):
-            fstage[g, q, :fq] = re[q * fq : (q + 1) * fq]
-            fstage[g, q, fq:] = im[q * fq : (q + 1) * fq]
+            fstage[u, q, :fq] = re[q * fq : (q + 1) * fq]
+            fstage[u, q, fq:] = im[q * fq : (q + 1) * fq]
 
     def coarse_peak(g):
         total = cstage[g, fx]
@@ -403,9 +432,9 @@
             total = total + frecv[g, k - 1]
         energy = total[:fq] * total[:fq] + total[fq:] * total[fq:]
         peak = energy
-        span = LANES // 2
-        while span >= 8:
-            peak = jnp.maximum(peak, pltpu.roll(peak, span, 1))
+        least, span = (2, LF) if g == groups else (8, LANES // 2)
+        while span >= least:
+            peak = jnp.maximum(peak, pltpu.roll(peak, LANES - span, 1))
             span //= 2
         peak = peak / fnorm[...]
         square = jnp.concatenate([peak, jnp.zeros((LANES - fq, LANES), jnp.float32)], axis=0)
@@ -420,70 +449,117 @@
         fnorm[...] = total[cq:]
         cres[...] = jnp.zeros_like(cres)
 
-    def give_back(g):
-        for p in range(4 * g, 4 * g + 4):
+    def give_back(u):
+        for p in units[u]:
             if p > 0:
                 r_move(p).start()
 
-    for g in range(groups):
-        here = (4 * g + 1, 4 * g + 2)
-        for p in here:
-            c_move(p).wait_recv()
-            if p + 2 <= nb - 1:
-                c_move(p + 2).start()
-        for c in range(parts):
+    def start_all(move, g):
+        for k in range(1, nf):
+            move(g, k).start()
+
+    def hop(h, unit=None, first=None):
+        here = [p for p in (2 * h - 1, 2 * h) if p <= nb - 1]
+        half = parts // 2
+        if unit is not None:
+            fpq[...] = jnp.zeros_like(fpq)
+
+        def part(i, carry):
+            c = (i % 2) * half + i // 2 if here == [nb - 1] else i
             for p in here:
                 f_move(p, c).wait_recv()
-                if p + 2 <= nb - 1 and not (p + 2 == nb - 1 and c >= parts // 2):
+                if p + 2 < nb - 1:
                     f_move(p + 2, c).start()
-                if p + 1 == nb - 1 and c >= parts // 2:
-                    f_move(p + 1, c).start()
+                elif p + 2 == nb - 1:
+
+                    @pl.when(c < half)
+                    def _():
+                        f_move(nb - 1, c, leftward=False).start()
+
+                elif p + 1 == nb - 1:
+
+                    @pl.when(c >= half)
+                    def _():
+                        f_move(nb - 1, c, leftward=True).start()
+
+            if first is not None:
+
+                @pl.when(i == 0)
+                def _():
+                    first()
+
+            if unit is not None:
+                fine_piece(unit, c)
+            return carry
+
+        lax.fori_loop(0, parts, part, 0)
+        if unit is not None:
+            fine_done(unit)
+            start_all(fx_move, unit)
+
+    def pass_coarse(h):
+        for p in (2 * h - 1, 2 * h):
+            if p <= nb - 1:
+                c_move(p).wait_recv()
+                if p + 2 <= nb - 1:
+                    c_move(p + 2).start()
+
+    if groups == 1:
+        powers()
+        single_phases()
+        for k in range(1, nf):
+            n_move(k).start()
+    for g in range(groups - 1):
+        hop(2 * g + 1, first=functools.partial(start_all, cx_move, g - 1) if g else None)
+        pass_coarse(2 * g + 1)
         if g == 0:
             powers()
         else:
             if g == 1:
                 norms()
-            coarse_peak(g - 1)
+                single_phases()
             fine_peak(g - 1)
             give_back(g - 1)
-        last = g == groups - 1
-        here = [p for p in (4 * g + 3, 4 * g + 4) if p <= nb - 1]
-        for p in here:
-            c_move(p).wait_recv()
-            if p + 2 <= nb - 1:
-                c_move(p + 2).start()
+            coarse_peak(g - 1)
+        hop(2 * g + 2, g)
+        pass_coarse(2 * g + 2)
+        if g == 0:
+            for k in range(1, nf):
+                n_move(k).start()
         coarse_group(g)
-        fpq[...] = jnp.zeros_like(fpq)
-
-        def piece(i, carry, g=g, here=here, last=last):
-            c = (i % 2) * (parts // 2) + i // 2 if last else i
-            for p in here:
-                f_move(p, c).wait_recv()
-                if not last:
-                    f_move(p + 2, c).start()
-            fine_piece(g, c)
-
-            @pl.when(i == 0)
-            def _():
-                for k in range(1, nf):
-                    cx_move(g, k).start()
-                if g == 0:
-                    for k in range(1, nf):
-                        n_move(k).start()
-
-            return carry
-
-        lax.fori_loop(0, parts, piece, 0)
-        fine_done(g)
-        for k in range(1, nf):
-            fx_move(g, k).start()
-    if groups == 1:
+    if groups == 2:
+        single_phases()
+    last = groups - 1
+    hop(2 * last + 1, last, functools.partial(start_all, cx_move, last - 1) if last else None)
+    pass_coarse(2 * last + 1)
+    hop(2 * last + 2, groups)
+    if groups <= 2:
         norms()
-    coarse_peak(groups - 1)
-    fine_peak(groups - 1)
-    give_back(groups - 1)
+    if last:
+        fine_peak(last - 1)
+        give_back(last - 1)
+    fine_peak(last)
+    give_back(last)
+    pass_coarse(2 * last + 2)
+    coarse_group(last)
+    fine_peak(groups)
+    give_back(groups)
+    start_all(cx_move, last)
+    rrecv[0] = rstage[0]
+    if last:
+        coarse_peak(last - 1)
+    for p in range(1, nb):
+        c_move(p).wait_send()
+        for c in range(parts):
+            f_move(p, c).wait_send()
+    for k in range(1, nf):
+        n_move(k).wait_send()
+        for g in range(groups + 1):
+            fx_move(g, k).wait_send()
+            if g < last:
+                cx_move(g, k).wait_send()
+    coarse_peak(last)
     coarse_out[...] = cres[...]
-    rrecv[0] = rstage[0]
     for p in range(1, nb):
         r_move(p).wait_recv()
 
@@ -498,22 +574,16 @@
             named.append(bank)
             away = lax.rem(me - bank + nb, nb)
             place = jnp.where(away < nb // 2, 2 * away, 2 * (nb - away) - 1)
-            row = lax.rem(place, 4) * 2 + rank
+            row = jnp.where(place == nb - 1, 0, lax.rem(place, 4) * 2) + rank
             tile = rrecv[place]
             line = jnp.sum(jnp.where(orow == row, tile, 0.0), axis=0, keepdims=True)
             result = jnp.where(orow == 2 * s + k, line, result)
     fine_out[...] = result
 
     for p in range(1, nb):
-        c_move(p).wait_send()
-        for c in range(parts):
-            f_move(p, c).wait_send()
         r_move(p).wait_send()
     for k in range(1, nf):
-        n_move(k).wait_send()
-        for g in range(groups):
-            cx_move(g, k).wait_send()
-            fx_move(g, k).wait_send()
+        cx_move(last, k).wait_send()
 
 
 def body(
@@ -538,7 +608,7 @@
     ccol, fcol = LC * 4 * segs, LF * 8
     f32, bf16 = jnp.float32, jnp.bfloat16
     dma = pltpu.SemaphoreType.DMA
-    anywhere = pl.BlockSpec(memory_space=pl.ANY)
+    anywhere = pl.BlockSpec(memory_space=pltpu.HBM)
     smem = pl.BlockSpec(memory_space=pltpu.SMEM)
     vmem = pl.BlockSpec(memory_space=pltpu.VMEM)
     coarse, fine = pl.pallas_call(
@@ -558,6 +628,7 @@
             pltpu.VMEM((2 * ftn, fbins), bf16),
             pltpu.VMEM((1, cbins), f32),
             pltpu.VMEM((1, fbins), f32),
+            pltpu.VMEM((2, 2 * LF, fbins), f32),
             pltpu.VMEM((8 * segs, cbins), f32),
             pltpu.VMEM((16, fbins // parts), f32),
             pltpu.VMEM((2, LC, cbins), f32),
@@ -566,18 +637,18 @@
             pltpu.VMEM((2 * fcol, min(DEEP, fbins // parts)), bf16),
             pltpu.VMEM((2 * ccol, 2 * ctn), f32),
             pltpu.VMEM((2 * fcol, 2 * ftn), f32),
-            pltpu.VMEM((groups, 16, 8 * segs), bf16),
-            pltpu.VMEM((groups, 8, LANES), jnp.int32),
+            pltpu.VMEM((groups + 1, 16, 8 * segs), bf16),
+            pltpu.VMEM((groups + 1, 8, LANES), jnp.int32),
             pltpu.VMEM((groups, nf, 2 * cq, ccol), f32),
             pltpu.VMEM((groups, nf - 1, 2 * cq, ccol), f32),
-            pltpu.VMEM((groups, nf, 2 * fq, fcol), f32),
-            pltpu.VMEM((groups, nf - 1, 2 * fq, fcol), f32),
+            pltpu.VMEM((groups + 1, nf, 2 * fq, fcol), f32),
+            pltpu.VMEM((groups + 1, nf - 1, 2 * fq, fcol), f32),
             pltpu.VMEM((nf, cq + fq, LANES), f32),
             pltpu.VMEM((nf - 1, cq + fq, LANES), f32),
             pltpu.VMEM((cq, LANES), f32),
             pltpu.VMEM((fq, LANES), f32),
             pltpu.VMEM((cq, LANES), f32),
-            pltpu.VMEM((groups, 8, LANES), f32),
+            pltpu.VMEM((groups + 1, 8, LANES), f32),
             pltpu.VMEM((nb, 8, LANES), f32),
             dma((2,)),
             dma((2,)),
@@ -591,13 +662,13 @@
             dma((nf - 1,)),
             dma((groups, nf - 1)),
             dma((groups, nf - 1)),
-            dma((groups, nf - 1)),
-            dma((groups, nf - 1)),
+            dma((groups + 1, nf - 1)),
+            dma((groups + 1, nf - 1)),
             dma((nb,)),
             dma((nb,)),
         ],
         compiler_params=pltpu.CompilerParams(
-            collective_id=0, has_side_effects=True, vmem_limit_bytes=67043328
+            collective_id=0, has_side_effects=True, vmem_limit_bytes=40 * 1024 * 1024
         ),
         name="search",
     )(

time: 98.7 us -> 106 us (1.074)
  local copies, waits for them, and re-layouts: 2.59 us -> 9.67 us
    unnamed x2 -> x18, local copies, waits for them, and re-layouts: 2.59 us -> 9.67 us
where the time goes in v3:
time: 106 us; the launch traced here: 105 us
  Pallas kernels  95 us (90%)
  local copies, waits for them, and re-layouts  9.67 us (9%)
    pallas_call x1, Pallas kernels, body(): pl.pallas_call(functools.partial(kernel, nb, nf), out_shape=(jax.ShapeDty...  95 us
    unnamed x18, local copies, waits for them, and re-layouts  9.67 us

profile of v3, /device:TPU:40, one launch (start us, length us, event | category | flops | bytes accessed | tf_op | source)
XLA Modules:
  0.0 105.3 jit_solution(13311247157630919490)
XLA Ops:
  0.6 0.0 copy-start
  0.6 2.2 %copy-done = bf16[2,1,64,16384]{3,2,1,0:T(8,128)(2,1)S(1)} copy-done((bf16[2,1,64,16384]{3,2,1,0:T(8,128)(2,1)S(1)}, bf16[2,1,64,16384]{3,2,1,0:T(8,128)(2,1)}, u32[]{:S(2)}) %copy-start) | copy-done | bytes 4194328
  2.8 0.0 copy-start.1
  2.8 1.6 %copy-done.1 = bf16[2,128,4096]{2,1,0:T(8,128)(2,1)S(1)} copy-done((bf16[2,128,4096]{2,1,0:T(8,128)(2,1)S(1)}, bf16[2,128,4096]{2,1,0:T(8,128)(2,1)}, u32[]{:S(2)}) %copy-start.1) | copy-done | bytes 2097176
  4.4 0.0 copy-start.2
  4.4 0.9 copy-done.2
  5.4 0.0 copy-start.3
  5.4 0.8 copy-done.3
  6.2 0.0 copy-start.4
  6.2 0.8 copy-done.4
  7.0 0.0 copy-start.5
  7.0 0.7 copy-done.5
  7.8 0.0 copy-start.6
  7.8 0.7 copy-done.6
  8.4 0.0 copy-start.7
  8.4 0.7 copy-done.7
  9.1 95.0 %search.1 = (f32[32,128]{1,0:T(8,128)S(1)}, f32[8,128]{1,0:T(8,128)S(1)}) custom-call(s32[2,64]{1,0:T(2,128)S(1)} %bitcast.15, s32[2,64]{1,0:T(2,128)S(1)} %bitcast.16, bf16[4,2,4096]{2,1,0:T(2,128)(2,1)S(1)} %copy-done.3, bf16[4,2,16384]{2,1,0:T(2,128)(2,1)S(1)} %copy-done.2, bf16[256,4096]{1,0:T(8,128)(2,1)S(1)} %bitcast.10, ...), custom_call_target="tpu_custom_call" | custom-call | tf_op jit(solution)/shard_map/search/pallas_call | solution.py:614
  104.1 0.6 copy.12
  104.7 0.6 copy.13
Async XLA Ops:
  0.6 2.2 %copy-start = (bf16[2,1,64,16384]{3,2,1,0:T(8,128)(2,1)S(1)}, bf16[2,1,64,16384]{3,2,1,0:T(8,128)(2,1)}, u32[]{:S(2)}) copy-start(bf16[2,1,64,16384]{3,2,1,0:T(8,128)(2,1)} %param.11) | copy-start | bytes 12582916
  2.8 1.6 %copy-start.1 = (bf16[2,128,4096]{2,1,0:T(8,128)(2,1)S(1)}, bf16[2,128,4096]{2,1,0:T(8,128)(2,1)}, u32[]{:S(2)}) copy-start(bf16[2,128,4096]{2,1,0:T(8,128)(2,1)} %param.10) | copy-start | bytes 6291460
  4.4 0.9 copy-start.2
  5.4 0.8 copy-start.3
  6.2 0.8 copy-start.4
  7.0 0.7 copy-start.5
  7.8 0.7 copy-start.6
  8.4 0.7 copy-start.7

commit v4 on v3

--- a/solution.py
+++ b/solution.py
@@ -58,7 +58,6 @@
     ft,
     cw,
     fw,
-    stab,
     cpure,
     fpure,
     ctab,
@@ -195,8 +194,6 @@
     load_fw.start()
     load_ct = pltpu.make_async_copy(ct_hbm, ct, ct_sem)
     load_ft = pltpu.make_async_copy(ft_hbm, ft, ft_sem)
-    load_ct.start()
-    load_ft.start()
 
     barrier = pltpu.get_barrier_semaphore()
     for neighbour in (left, right):
@@ -205,6 +202,8 @@
         pl.semaphore_signal(barrier, inc=1, device_id={"freq": other(k)}, device_id_type=MESH)
     own_c.wait()
     own_f.wait()
+    load_ct.start()
+    load_ft.start()
 
     def settle(raw, buf, begin, size):
         for at in range(begin, begin + size, STEP):
@@ -248,19 +247,6 @@
         return carry
 
     lax.fori_loop(0, fbins // STEP, f_phases, 0)
-
-    def single_phases():
-        def step(i, carry):
-            at = pl.ds(pl.multiple_of(i * STEP, STEP), STEP)
-            lag = lax.broadcasted_iota(jnp.int32, (2 * LF, STEP), 0) // 2
-            f = fx * fbins + i * STEP + lax.broadcasted_iota(jnp.int32, (2 * LF, STEP), 1)
-            cos, sin = unit_phase((f * lag) & (PERIOD - 1))
-            w = fw[:, at]
-            stab[0, :, at] = cos * w
-            stab[1, :, at] = sin * w
-            return carry
-
-        lax.fori_loop(0, fbins // STEP, step, 0)
 
     rows = lax.broadcasted_iota(jnp.int32, (16, 8 * segs), 0)
     cols = lax.broadcasted_iota(jnp.int32, (16, 8 * segs), 1)
@@ -276,11 +262,11 @@
                 for k in range(2):
                     hit = jnp.where(trig[k, base + s] == me, 1, 0)
                     slot = 2 * i + found
-                    row = (rows & 7) & 1 if u == groups else rows & 7
+                    row = (rows & 7) >> 2 if u == groups else rows & 7
                     col = (i * segs + s) * 2
                     here = (row == slot) & (cols == col + (rows >> 3))
                     pick += jnp.where(here, hit.astype(jnp.float32), 0.0)
-                    shift += jnp.where((orow & 1 if u == groups else orow) == slot, hit * offs[k, base + s], 0)
+                    shift += jnp.where((orow >> 2 if u == groups else orow) == slot, hit * offs[k, base + s], 0)
                     found = found + hit
         sel[u] = pick.astype(jnp.bfloat16)
         soff[u] = shift
@@ -294,7 +280,7 @@
             im = ct[ctn:, at].astype(jnp.float32)
             return total + (re * re + im * im) * cw[:, at]
 
-        ct_sum = lax.fori_loop(0, cbins // LANES, c_power, jnp.zeros((ctn, LANES), jnp.float32))
+        ct_sum = lax.fori_loop(0, cbins // LANES, c_power, jnp.zeros((ctn, LANES), jnp.float32), unroll=2)
         ct_sum = jnp.broadcast_to(jnp.sum(ct_sum, axis=1, keepdims=True), (ctn, LANES))
         load_ft.wait()
 
@@ -304,7 +290,7 @@
             im = ft[ftn:, at].astype(jnp.float32)
             return total + (re * re + im * im) * fw[:, at]
 
-        ft_sum = lax.fori_loop(0, fbins // LANES, f_power, jnp.zeros((ftn, LANES), jnp.float32))
+        ft_sum = lax.fori_loop(0, fbins // LANES, f_power, jnp.zeros((ftn, LANES), jnp.float32), unroll=4)
         ft_sum = jnp.broadcast_to(jnp.sum(ft_sum, axis=1, keepdims=True), (ftn, LANES))
         for q in range(nf):
             nstage[q, :cq] = ct_sum[q * cq : (q + 1) * cq]
@@ -348,7 +334,7 @@
     def fine_piece(u, c):
         single = u == groups
         ncol = LF * (2 if single else 8)
-        table = stab if single else ftab
+        low = lax.broadcasted_iota(jnp.int32, (8, 2 * LANES), 0) < 4
         places = units[u] + (units[groups - 1] if single else [])
         places = (places + places)[:4]
         wide = min(2 * STEP, fpart)
@@ -374,11 +360,19 @@
                 at = pl.ds(whole + kt, 2 * LANES)
                 here = slice(kt, kt + 2 * LANES)
                 for j in range(0, ncol // 8, 2):
+                    if single:
+                        pair = []
+                        for part in range(2):
+                            rows8 = ftab[part, j * 4 : j * 4 + 8, at]
+                            turned = pltpu.roll(rows8, 4, 0)
+                            pair.append((jnp.where(low, rows8, turned), jnp.where(low, turned, rows8)))
                     res, ims = [], []
-                    for jj in (j, j + 1):
-                        lag = slice(jj * 8, jj * 8 + 8) if single else slice(jj, jj + 1)
-                        wc = table[0, lag, at]
-                        ws = table[1, lag, at]
+                    for jj in range(2):
+                        if single:
+                            wc, ws = pair[0][jj], pair[1][jj]
+                        else:
+                            wc = ftab[0, j + jj : j + jj + 1, at]
+                            ws = ftab[1, j + jj : j + jj + 1, at]
                         res.append(sr * wc - si * ws)
                         ims.append(sr * ws + si * wc)
                     flag[j * 8 : j * 8 + 16, here] = jnp.concatenate(res, axis=0).astype(jnp.bfloat16)
@@ -432,10 +426,8 @@
             total = total + frecv[g, k - 1]
         energy = total[:fq] * total[:fq] + total[fq:] * total[fq:]
         peak = energy
-        least, span = (2, LF) if g == groups else (8, LANES // 2)
-        while span >= least:
+        for span in (16, 8, 2, 1) if g == groups else (64, 32, 16, 8):
             peak = jnp.maximum(peak, pltpu.roll(peak, LANES - span, 1))
-            span //= 2
         peak = peak / fnorm[...]
         square = jnp.concatenate([peak, jnp.zeros((LANES - fq, LANES), jnp.float32)], axis=0)
         rstage[g] = square.T[:8]
@@ -506,7 +498,6 @@
 
     if groups == 1:
         powers()
-        single_phases()
         for k in range(1, nf):
             n_move(k).start()
     for g in range(groups - 1):
@@ -517,7 +508,6 @@
         else:
             if g == 1:
                 norms()
-                single_phases()
             fine_peak(g - 1)
             give_back(g - 1)
             coarse_peak(g - 1)
@@ -527,27 +517,38 @@
             for k in range(1, nf):
                 n_move(k).start()
         coarse_group(g)
-    if groups == 2:
-        single_phases()
     last = groups - 1
     hop(2 * last + 1, last, functools.partial(start_all, cx_move, last - 1) if last else None)
     pass_coarse(2 * last + 1)
     hop(2 * last + 2, groups)
     if groups <= 2:
         norms()
+    pass_coarse(2 * last + 2)
+    coarse_group(last)
     if last:
         fine_peak(last - 1)
         give_back(last - 1)
+    start_all(cx_move, last)
     fine_peak(last)
     give_back(last)
-    pass_coarse(2 * last + 2)
-    coarse_group(last)
     fine_peak(groups)
     give_back(groups)
-    start_all(cx_move, last)
     rrecv[0] = rstage[0]
     if last:
         coarse_peak(last - 1)
+
+    spots, named = [], []
+    for s in range(segs):
+        for k in range(2):
+            bank = trig[k, me * segs + s]
+            rank = jnp.int32(0)
+            for before in named:
+                rank = rank + jnp.where(before == bank, 1, 0)
+            named.append(bank)
+            away = lax.rem(me - bank + nb, nb)
+            place = jnp.where(away < nb // 2, 2 * away, 2 * (nb - away) - 1)
+            row = jnp.where(place == nb - 1, 4 * rank, lax.rem(place, 4) * 2 + rank)
+            spots.append((jnp.clip(place, 0, nb - 1), jnp.clip(row, 0, 7)))
     for p in range(1, nb):
         c_move(p).wait_send()
         for c in range(parts):
@@ -558,32 +559,21 @@
             fx_move(g, k).wait_send()
             if g < last:
                 cx_move(g, k).wait_send()
+    for p in range(1, nb - 4):
+        r_move(p).wait_send()
     coarse_peak(last)
     coarse_out[...] = cres[...]
+    for k in range(1, nf):
+        cx_move(last, k).wait_send()
+    for p in range(max(1, nb - 4), nb):
+        r_move(p).wait_send()
     for p in range(1, nb):
         r_move(p).wait_recv()
-
     result = jnp.zeros((8, LANES), jnp.float32)
-    named = []
-    for s in range(segs):
-        for k in range(2):
-            bank = trig[k, me * segs + s]
-            rank = jnp.int32(0)
-            for before in named:
-                rank = rank + jnp.where(before == bank, 1, 0)
-            named.append(bank)
-            away = lax.rem(me - bank + nb, nb)
-            place = jnp.where(away < nb // 2, 2 * away, 2 * (nb - away) - 1)
-            row = jnp.where(place == nb - 1, 0, lax.rem(place, 4) * 2) + rank
-            tile = rrecv[place]
-            line = jnp.sum(jnp.where(orow == row, tile, 0.0), axis=0, keepdims=True)
-            result = jnp.where(orow == 2 * s + k, line, result)
+    for n, (place, row) in enumerate(spots):
+        line = rrecv[place, pl.ds(row, 1), :]
+        result = jnp.where(orow == n, line, result)
     fine_out[...] = result
-
-    for p in range(1, nb):
-        r_move(p).wait_send()
-    for k in range(1, nf):
-        cx_move(last, k).wait_send()
 
 
 def body(
@@ -608,7 +598,7 @@
     ccol, fcol = LC * 4 * segs, LF * 8
     f32, bf16 = jnp.float32, jnp.bfloat16
     dma = pltpu.SemaphoreType.DMA
-    anywhere = pl.BlockSpec(memory_space=pltpu.HBM)
+    anywhere = pl.BlockSpec(memory_space=pl.ANY)
     smem = pl.BlockSpec(memory_space=pltpu.SMEM)
     vmem = pl.BlockSpec(memory_space=pltpu.VMEM)
     coarse, fine = pl.pallas_call(
@@ -628,7 +618,6 @@
             pltpu.VMEM((2 * ftn, fbins), bf16),
             pltpu.VMEM((1, cbins), f32),
             pltpu.VMEM((1, fbins), f32),
-            pltpu.VMEM((2, 2 * LF, fbins), f32),
             pltpu.VMEM((8 * segs, cbins), f32),
             pltpu.VMEM((16, fbins // parts), f32),
             pltpu.VMEM((2, LC, cbins), f32),
@@ -668,7 +657,7 @@
             dma((nb,)),
         ],
         compiler_params=pltpu.CompilerParams(
-            collective_id=0, has_side_effects=True, vmem_limit_bytes=40 * 1024 * 1024
+            collective_id=0, has_side_effects=True, vmem_limit_bytes=67043328
         ),
         name="search",
     )(

time: 106 us -> 96 us (0.906)
  local copies, waits for them, and re-layouts: 9.67 us -> 2.59 us
  Pallas kernels: 95 us -> 92.5 us
    unnamed x18 -> x2, local copies, waits for them, and re-layouts: 9.67 us -> 2.59 us
    pallas_call x1, Pallas kernels: 95 us -> 92.5 us  [body(): pl.pallas_call(functools.partial(kernel, nb, nf), out_shape=(jax.ShapeDty...]
where the time goes in v4:
time: 96 us; the launch traced here: 95.7 us
  Pallas kernels  92.5 us (96%)
  local copies, waits for them, and re-layouts  2.59 us (3%)
    pallas_call x1, Pallas kernels, body(): pl.pallas_call(functools.partial(kernel, nb, nf), out_shape=(jax.ShapeDty...  92.5 us
    unnamed x2, local copies, waits for them, and re-layouts  2.59 us

profile of v4, /device:TPU:40, one launch (start us, length us, event | category | flops | bytes accessed | tf_op | source)
XLA Modules:
  0.0 95.7 jit_solution(6366663781363652073)
XLA Ops:
  0.6 92.5 %search.1 = (f32[32,128]{1,0:T(8,128)}, f32[8,128]{1,0:T(8,128)}) custom-call(s32[2,64]{1,0:T(2,128)} %bitcast.15, s32[2,64]{1,0:T(2,128)} %bitcast.16, bf16[4,2,4096]{2,1,0:T(2,128)(2,1)} %cs_hbm.1, bf16[4,2,16384]{2,1,0:T(2,128)(2,1)} %fs_hbm.1, bf16[256,4096]{1,0:T(8,128)(2,1)} %bitcast.10, bf16[128,16384]{1,0:T(8,128)(2,1)} %bitcast.9, ...), custom_call_target="tpu_custom_call" | custom-call | tf_op jit(solution)/shard_map/search/pallas_call | solution.py:604
  93.1 1.3 %copy.12 = f32[32,64]{1,0:T(8,128)} copy(f32[32,64]{1,0:T(8,128)} %bitcast.13) | data formatting | bytes 16384
  94.4 1.3 %copy.13 = f32[4,2,16]{2,1,0:T(2,128)} copy(f32[4,2,16]{2,1,0:T(2,128)} %bitcast.14) | data formatting | bytes 1024

commit v5 on v4

--- a/solution.py
+++ b/solution.py
@@ -349,7 +349,7 @@
             yr, yi = y[:8], y[8:]
             fpure[:8, begin : begin + wide] = yr * cos - yi * sin
             fpure[8:, begin : begin + wide] = yr * sin + yi * cos
-        deep = min(DEEP, fpart)
+        deep = fpart if single else min(DEEP, fpart)
 
         def step(i, carry):
             base = pl.multiple_of(i * deep, deep)
@@ -378,7 +378,7 @@
                     flag[j * 8 : j * 8 + 16, here] = jnp.concatenate(res, axis=0).astype(jnp.bfloat16)
                     flag[ncol + j * 8 : ncol + j * 8 + 16, here] = jnp.concatenate(ims, axis=0).astype(jnp.bfloat16)
             fpq[: 2 * ncol] += lax.dot_general(
-                flag[: 2 * ncol], ft[:, pl.ds(whole, deep)], NT, preferred_element_type=jnp.float32
+                flag[: 2 * ncol, :deep], ft[:, pl.ds(whole, deep)], NT, preferred_element_type=jnp.float32
             )
             return carry
 
@@ -525,10 +525,10 @@
         norms()
     pass_coarse(2 * last + 2)
     coarse_group(last)
+    start_all(cx_move, last)
     if last:
         fine_peak(last - 1)
         give_back(last - 1)
-    start_all(cx_move, last)
     fine_peak(last)
     give_back(last)
     fine_peak(groups)
@@ -623,7 +623,7 @@
             pltpu.VMEM((2, LC, cbins), f32),
             pltpu.VMEM((2, LF, fbins), f32),
             pltpu.VMEM((2 * ccol, min(DEEP, cbins)), bf16),
-            pltpu.VMEM((2 * fcol, min(DEEP, fbins // parts)), bf16),
+            pltpu.VMEM((2 * fcol, fbins // parts), bf16),
             pltpu.VMEM((2 * ccol, 2 * ctn), f32),
             pltpu.VMEM((2 * fcol, 2 * ftn), f32),
             pltpu.VMEM((groups + 1, 16, 8 * segs), bf16),
@@ -657,7 +657,7 @@
             dma((nb,)),
         ],
         compiler_params=pltpu.CompilerParams(
-            collective_id=0, has_side_effects=True, vmem_limit_bytes=67043328
+            collective_id=0, has_side_effects=True, vmem_limit_bytes=55200 * 1024
         ),
         name="search",
     )(

time: 96 us -> 94.4 us (0.983)
  Pallas kernels: 92.5 us -> 91 us
    pallas_call x1, Pallas kernels: 92.5 us -> 91 us  [body(): pl.pallas_call(functools.partial(kernel, nb, nf), out_shape=(jax.ShapeDty...]
    unnamed x2 -> x6, local copies, waits for them, and re-layouts: 2.59 us -> 2.55 us
where the time goes in v5:
time: 94.4 us; the launch traced here: 94.2 us
  Pallas kernels  91 us (96%)
  local copies, waits for them, and re-layouts  2.55 us (3%)
    pallas_call x1, Pallas kernels, body(): pl.pallas_call(functools.partial(kernel, nb, nf), out_shape=(jax.ShapeDty...  91 us
    unnamed x6, local copies, waits for them, and re-layouts  2.55 us

profile of v5, /device:TPU:40, one launch (start us, length us, event | category | flops | bytes accessed | tf_op | source)
XLA Modules:
  0.0 94.2 jit_solution(508723066184646823)
XLA Ops:
  0.6 0.0 copy-start
  0.6 0.7 copy-done
  1.3 0.0 copy-start.1
  1.3 0.7 copy-done.1
  2.0 91.0 %search.1 = (f32[32,128]{1,0:T(8,128)S(1)}, f32[8,128]{1,0:T(8,128)S(1)}) custom-call(s32[2,64]{1,0:T(2,128)S(1)} %bitcast.11, s32[2,64]{1,0:T(2,128)S(1)} %bitcast.12, bf16[4,2,4096]{2,1,0:T(2,128)(2,1)} %cs_hbm.1, bf16[4,2,16384]{2,1,0:T(2,128)(2,1)} %fs_hbm.1, bf16[256,4096]{1,0:T(8,128)(2,1)} %bitcast.14, bf16[128,16384]{1,0:T(8,128)(2,1)} %bitcast.13, ...), custom_call_target="tpu_custom_call" | custom-call | tf_op jit(solution)/shard_map/search/pallas_call | solution.py:604
  93.0 0.6 copy.12
  93.6 0.6 copy.13
Async XLA Ops:
  0.6 0.7 copy-start
  1.3 0.7 copy-start.1

commit v6 on v5

--- a/solution.py
+++ b/solution.py
@@ -40,8 +40,7 @@
 def kernel(
     nb,
     nf,
-    trig,
-    offs,
+    marks,
     cs_hbm,
     fs_hbm,
     ct_hbm,
@@ -109,6 +108,7 @@
     cq = ctn // nf
     fq = ftn // nf
     scale = PERIOD // (2 * FC)
+    shift_bits = nb.bit_length() - 1
 
     def source(p):
         step = (nb - (p + 1) // 2) if p % 2 else p // 2
@@ -185,9 +185,14 @@
         )
 
     own_c = pltpu.make_async_copy(cs_hbm, craw, load_sem.at[0])
-    own_f = pltpu.make_async_copy(fs_hbm, fraw, load_sem.at[1])
+
+    def own_f(c):
+        part = pl.ds(c * fpart, fpart)
+        return pltpu.make_async_copy(fs_hbm.at[:, :, part], fraw.at[:, :, part], load_sem.at[c + 1])
+
+    for c in range(parts):
+        own_f(c).start()
     own_c.start()
-    own_f.start()
     load_cw = pltpu.make_async_copy(cw_hbm, cw, w_sem.at[0])
     load_fw = pltpu.make_async_copy(fw_hbm, fw, w_sem.at[1])
     load_cw.start()
@@ -200,27 +205,28 @@
         pl.semaphore_signal(barrier, inc=1, device_id={"bank": neighbour}, device_id_type=MESH)
     for k in range(1, nf):
         pl.semaphore_signal(barrier, inc=1, device_id={"freq": other(k)}, device_id_type=MESH)
-    own_c.wait()
-    own_f.wait()
-    load_ct.start()
-    load_ft.start()
 
     def settle(raw, buf, begin, size):
         for at in range(begin, begin + size, STEP):
             piece = [raw[r, :, at : at + STEP].astype(jnp.float32) for r in range(segs)]
             buf[0, :, at : at + STEP] = jnp.concatenate(piece, axis=0).astype(jnp.bfloat16)
 
+    own_f(0).wait()
     settle(fraw, fbuf, 0, fpart)
     pl.semaphore_wait(barrier, 2 + nf - 1)
     for c in range(parts):
         if c + 1 < parts:
+            own_f(c + 1).wait()
             settle(fraw, fbuf, (c + 1) * fpart, fpart)
         else:
+            own_c.wait()
             settle(craw, cbuf, 0, cbins)
         for p in (1, 2):
             f_move(p, c).start()
     for p in (1, 2):
         c_move(p).start()
+    load_ct.start()
+    load_ft.start()
     load_cw.wait()
     load_fw.wait()
 
@@ -260,13 +266,14 @@
             found = jnp.int32(0)
             for s in range(segs):
                 for k in range(2):
-                    hit = jnp.where(trig[k, base + s] == me, 1, 0)
+                    mark = marks[k, base + s]
+                    hit = jnp.where((mark & (nb - 1)) == me, 1, 0)
                     slot = 2 * i + found
                     row = (rows & 7) >> 2 if u == groups else rows & 7
                     col = (i * segs + s) * 2
                     here = (row == slot) & (cols == col + (rows >> 3))
                     pick += jnp.where(here, hit.astype(jnp.float32), 0.0)
-                    shift += jnp.where((orow >> 2 if u == groups else orow) == slot, hit * offs[k, base + s], 0)
+                    shift += jnp.where((orow >> 2 if u == groups else orow) == slot, hit * (mark >> shift_bits), 0)
                     found = found + hit
         sel[u] = pick.astype(jnp.bfloat16)
         soff[u] = shift
@@ -540,7 +547,7 @@
     spots, named = [], []
     for s in range(segs):
         for k in range(2):
-            bank = trig[k, me * segs + s]
+            bank = marks[k, me * segs + s] & (nb - 1)
             rank = jnp.int32(0)
             for before in named:
                 rank = rank + jnp.where(before == bank, 1, 0)
@@ -607,7 +614,7 @@
             jax.ShapeDtypeStruct((cq, LANES), f32),
             jax.ShapeDtypeStruct((8, LANES), f32),
         ),
-        in_specs=[smem, smem] + [anywhere] * 6,
+        in_specs=[smem] + [anywhere] * 6,
         out_specs=(vmem, vmem),
         scratch_shapes=[
             pltpu.VMEM((segs, 2, cbins), bf16),
@@ -639,7 +646,7 @@
             pltpu.VMEM((cq, LANES), f32),
             pltpu.VMEM((groups + 1, 8, LANES), f32),
             pltpu.VMEM((nb, 8, LANES), f32),
-            dma((2,)),
+            dma((parts + 1,)),
             dma((2,)),
             dma,
             dma,
@@ -661,8 +668,7 @@
         ),
         name="search",
     )(
-        triggers.T,
-        offsets.T,
+        (offsets * nb + triggers).T,
         coarse_spectra,
         fine_spectra,
         coarse_templates.reshape(2 * ctn, cbins),

time: 94.4 us -> 93.7 us (level)
  local copies, waits for them, and re-layouts: 2.55 us -> 1.2 us
    unnamed x6 -> x2, local copies, waits for them, and re-layouts: 2.55 us -> 1.2 us
where the time goes in v6:
time: 93.7 us; the launch traced here: 93.6 us
  Pallas kernels  91 us (97%)
  local copies, waits for them, and re-layouts  1.2 us (1%)
    pallas_call x1, Pallas kernels, body(): pl.pallas_call(functools.partial(kernel, nb, nf), out_shape=(jax.ShapeDty...  91 us

profile of v6, /device:TPU:40, one launch (start us, length us, event | category | flops | bytes accessed | tf_op | source)
XLA Modules:
  0.0 93.6 jit_solution(2043894797512940980)
XLA Ops:
  0.6 0.7 add_bitcast_fusion.marks
  1.3 91.0 %search.1 = (f32[32,128]{1,0:T(8,128)S(1)}, f32[8,128]{1,0:T(8,128)S(1)}) custom-call(s32[2,64]{1,0:T(2,128)S(1)} %add_bitcast_fusion.marks, bf16[4,2,4096]{2,1,0:T(2,128)(2,1)} %cs_hbm.1, bf16[4,2,16384]{2,1,0:T(2,128)(2,1)} %fs_hbm.1, bf16[256,4096]{1,0:T(8,128)(2,1)} %bitcast.12, bf16[128,16384]{1,0:T(8,128)(2,1)} %bitcast.11, f32[1,4096]{1,0:T(1,128)} %bitcast.14, ...), custom_call_target="tpu_custom_call" | custom-call | tf_op jit(solution)/shard_map/search/pallas_call | solution.py:611
  92.4 0.6 copy.12
  93.0 0.6 copy.13
